TPU v7x, 256 devices: a whole 4x4x8 slice. The times are simulated.
256 devices in a mesh: gx: 16 (over z_hi, x, core), gy: 16 (over y, z_lo).
Axes of the slice: x: 4, y: 4, z: 8 (z_hi: 2, z_lo: 4; z = z_hi * 4 + z_lo), core: 2. Of those that a mesh axis runs over, the one named last changes fastest.
Arguments:
- right_side: float32 [2, 256, 512, 128], P(None, 'gx', 'gy'), may hold values from -6 to 6
- wavenumber: float32 [256, 512, 128], P('gx', 'gy'), may hold values from 0.2 to 1
- pml_layer: int32 [256, 512, 128], P('gx', 'gy'), may hold values from 0 to 3
- aggregate: int32 [256, 512, 128], P('gx', 'gy'), may hold values from 0 to 15, as said below
- coarse_inverse: float32 [2, 4096, 4096], P(None, ('gx', 'gy')), may hold values from -0.0009765625 to 0.0009765625
Outputs:
- solution: float32 [2, 256, 512, 128], P(None, 'gx', 'gy')
- hessenberg: float32 [2, 5, 4], replicated
Inputs may be any that keep to these rules, and one draw needn't show every extreme that they name: `aggregate`: along the third dimension the value never falls, and every value of 0 to 15 occurs in every column of cells.
All inputs are finite; a program needn't handle non-finite values.
Results may differ from a plain program's by a relative error of at most 0.00015.
Values sent between devices are 32-bit elements; how exact they have to be, the bound alone decides.
A program may use at most 64 MiB of HBM per device.

v0:
```python
import functools
import math

import jax
import jax.numpy as jnp
from jax import lax
from jax.sharding import Mesh
from jax.sharding import PartitionSpec as P

ITERS = 4
GX_GY = ("gx_0", "gx_1", "gx_2", "gy_0", "gy_1")
GX = ("gx_0", "gx_1", "gx_2")
GY = ("gy_0", "gy_1")


damping = 0.8
pml_strength = 3.0
epsilon = 1e-06


def edges_of(length, count):
    turn = length // count
    if turn >= 8:
        turn -= turn % 8
    return [turn * k for k in range(1, count)]


def stacked_from(x, axes, turns):
    pieces = x
    for k in turns:
        pieces = lax.all_gather(pieces, axes[k])
    done = turns[::-1]
    back = [done.index(k) for k in range(len(axes))]
    pieces = pieces.transpose(*back, *range(len(axes), pieces.ndim))
    return pieces.reshape(-1, *x.shape)


def laid_out(pieces, dim):
    pieces = jnp.moveaxis(pieces, 0, dim)
    dims = pieces.shape
    return pieces.reshape(*dims[:dim], dims[dim] * dims[dim + 1], *dims[dim + 2 :])


def spread_gather(x, axes, dim):
    widest = max(range(max(1, x.ndim - 1)), key=lambda d: x.shape[d])
    count, outs = (len(axes), [])
    for first, piece in enumerate(jnp.split(x, edges_of(x.shape[widest], count), axis=widest)):
        if piece.size:
            turns = [(first - k) % count for k in range(count)]
            outs.append(stacked_from(piece, axes, turns))
    return laid_out(jnp.concatenate(outs, axis=widest + 1), dim)


def with_halo(x, sides, width):
    edges = {}
    for axis, dim in sides:
        devices, length = (lax.axis_size(axis), x.shape[dim])
        up = [(i, (i + 1) % devices) for i in range(devices - 1)]
        last = lax.slice_in_dim(x, length - width, length, axis=dim)
        first = lax.slice_in_dim(x, 0, width, axis=dim)
        edges[dim] = (
            lax.ppermute(last, axis, up),
            lax.ppermute(first, axis, [(b, a) for a, b in up]),
        )
    done = []
    for _, dim in sides:
        low, high = edges[dim]
        around = [(width, width) if d in done else (0, 0) for d in range(x.ndim)]
        x = jnp.concatenate([jnp.pad(low, around), x, jnp.pad(high, around)], axis=dim)
        done.append(dim)
    return x


def with_halo_2(block, sides, width):
    for axis, dim in sides:
        count = lax.axis_size(axis)
        forward = [(i, i + 1) for i in range(count - 1)]
        backward = [(target, source) for source, target in forward]
        low = lax.ppermute(
            lax.slice_in_dim(block, block.shape[dim] - width, None, axis=dim), axis, forward
        )
        high = lax.ppermute(lax.slice_in_dim(block, 0, width, axis=dim), axis, backward)
        block = jnp.concatenate([low, block, high], axis=dim)
    return block


def by_axis(x, axes):
    return functools.reduce(lax.psum, axes, x)


def coefficients(wavenumber, layer_float):
    wave_sq = wavenumber * wavenumber
    depth = layer_float / 3.0
    absorb = wave_sq * (pml_strength * depth * depth)
    diag_re = 6.0 - wave_sq
    magnitude = diag_re * diag_re + absorb * absorb
    return (wave_sq, absorb, damping * diag_re / magnitude, damping * absorb / magnitude)


def operate_inner(extended, wave_sq, absorb):
    middle = extended[:, 1:-1, 1:-1]
    above = jnp.concatenate([middle[..., 1:], jnp.zeros_like(middle[..., :1])], -1)
    below = jnp.concatenate([jnp.zeros_like(middle[..., :1]), middle[..., :-1]], -1)
    beside = (
        extended[:, 2:, 1:-1]
        + extended[:, :-2, 1:-1]
        + extended[:, 1:-1, 2:]
        + extended[:, 1:-1, :-2]
        + above
        + below
    )
    real_part = (6.0 - wave_sq) * middle[0] - beside[0] + absorb * middle[1]
    imag_part = (6.0 - wave_sq) * middle[1] - beside[1] - absorb * middle[0]
    return jnp.stack([real_part, imag_part])


def smooth(field, scale_re, scale_im):
    return jnp.stack(
        [scale_re * field[0] - scale_im * field[1], scale_re * field[1] + scale_im * field[0]]
    )


def complex_scale(scale_re, scale_im, field):
    return jnp.stack(
        [scale_re * field[0] - scale_im * field[1], scale_re * field[1] + scale_im * field[0]]
    )


def inner_local(left, right):
    return jnp.stack(
        [
            jnp.sum(left[0] * right[0] + left[1] * right[1]),
            jnp.sum(left[0] * right[1] - left[1] * right[0]),
        ]
    )


def least_squares(hessenberg, beta):
    real_h = hessenberg[0]
    imag_h = hessenberg[1]
    stacked = jnp.concatenate(
        [jnp.concatenate([real_h, -imag_h], 1), jnp.concatenate([imag_h, real_h], 1)], 0
    )
    count = stacked.shape[1]
    target = jnp.zeros((stacked.shape[0],), jnp.float32).at[0].set(beta)
    ortho = []
    upper = {}
    for column in range(count):
        vector = stacked[:, column]
        for position in range(column):
            upper[position, column] = jnp.zeros((), jnp.float32)
        for repeat in range(2):
            for position in range(len(ortho)):
                weight = jnp.sum(ortho[position] * vector)
                vector = vector - weight * ortho[position]
                upper[position, column] = upper[position, column] + weight
        norm_value = jnp.sqrt(jnp.sum(vector * vector))
        upper[column, column] = norm_value
        ortho.append(vector / norm_value)
    project = [jnp.sum(basis_vec * target) for basis_vec in ortho]
    solved = [None] * count
    for column in reversed(range(count)):
        total = project[column]
        for later in range(column + 1, count):
            total = total - upper[column, later] * solved[later]
        solved[column] = total / upper[column, column]
    return solved


def restrict(flat_field, flat_ids, levels_count):
    total = flat_ids.shape[0]
    block = math.gcd(total, 16384)
    levels = jnp.arange(levels_count, dtype=jnp.int32)

    def accumulate(step_index, result):
        piece = lax.dynamic_slice_in_dim(flat_field, step_index * block, block, 1)
        labels = lax.dynamic_slice_in_dim(flat_ids, step_index * block, block, 0)
        onehot = (labels[None, :] == levels[:, None]).astype(jnp.float32)
        return result + lax.dot_general(
            piece, onehot, (((1,), (1,)), ((), ())), precision=lax.Precision.HIGHEST
        )

    return lax.fori_loop(0, total // block, accumulate, jnp.zeros((2, levels_count), jnp.float32))


def prolong(values, flat_ids):
    total = flat_ids.shape[0]
    block = math.gcd(total, 16384)
    levels = jnp.arange(values.shape[1], dtype=jnp.int32)

    def place(step_index, result):
        labels = lax.dynamic_slice_in_dim(flat_ids, step_index * block, block, 0)
        onehot = (levels[:, None] == labels[None, :]).astype(jnp.float32)
        piece = jnp.dot(values, onehot, precision=lax.Precision.HIGHEST)
        return lax.dynamic_update_slice_in_dim(result, piece, step_index * block, 1)

    return lax.fori_loop(0, total // block, place, jnp.zeros((2, total), jnp.float32))


def coarse_fix(remainder, flat_ids, coarse_inverse):
    highest = lax.Precision.HIGHEST
    levels_count = coarse_inverse.shape[1]
    partial_value = restrict(remainder.reshape(2, -1), flat_ids, levels_count)
    whole = spread_gather(partial_value, GX_GY, 1)
    own_re = jnp.dot(coarse_inverse[0], whole[0], precision=highest) - jnp.dot(
        coarse_inverse[1], whole[1], precision=highest
    )
    own_im = jnp.dot(coarse_inverse[0], whole[1], precision=highest) + jnp.dot(
        coarse_inverse[1], whole[0], precision=highest
    )
    return prolong(jnp.stack([own_re, own_im]), flat_ids).reshape(remainder.shape)


def operate_final(field, wave_sq, absorb):
    extended = with_halo(field, ((GX, 1), (GY, 2)), 1)
    return operate_inner(extended, wave_sq, absorb)


def smooth_wide(vector, wide_coef, inside, wave_sq, absorb):
    wide_sq, wide_abs, wide_re, wide_im = wide_coef
    extended = with_halo_2(vector, ((GX, 1), (GY, 2)), 2)
    first = smooth(extended, wide_re, wide_im)
    image = operate_inner(first, wide_sq[1:-1, 1:-1], wide_abs[1:-1, 1:-1])
    second = (
        first[:, 1:-1, 1:-1]
        + smooth(extended[:, 1:-1, 1:-1] - image, wide_re[1:-1, 1:-1], wide_im[1:-1, 1:-1])
    ) * inside[1:-1, 1:-1]
    remainder = vector - operate_inner(second, wave_sq, absorb)
    return (second[:, 1:-1, 1:-1], remainder)


def body(right_side, wavenumber, pml_layer, aggregate, coarse_inverse):
    layer_float = pml_layer.astype(jnp.float32)
    wave_sq, absorb, scale_re, scale_im = coefficients(wavenumber, layer_float)
    flat_ids = aggregate.reshape(-1)
    stacked = jnp.stack([wavenumber, layer_float, jnp.ones_like(wavenumber)])
    wide = with_halo_2(stacked, ((GX, 1), (GY, 2)), 2)
    wide_coef = coefficients(wide[0], wide[1])
    inside = wide[2]
    beta = jnp.sqrt(by_axis(jnp.sum(right_side * right_side), GX_GY) + epsilon)
    basis = [right_side / beta]
    directions = []
    columns_re = []
    columns_im = []
    for column in range(ITERS):
        vector = basis[column]
        second, remainder = smooth_wide(vector, wide_coef, inside, wave_sq, absorb)
        direction = second + coarse_fix(remainder, flat_ids, coarse_inverse)
        image = operate_final(direction, wave_sq, absorb)
        local_dots = jnp.stack([inner_local(member, image) for member in basis], 1)
        dots, squared = (by_axis(local_dots, GX_GY), by_axis(jnp.sum(image * image), GX_GY))
        for position in range(len(basis)):
            image = image - complex_scale(dots[0, position], dots[1, position], basis[position])
        leftover = squared - jnp.sum(dots * dots)
        length = jnp.sqrt(jnp.maximum(leftover, 0.0) + epsilon)
        tail = jnp.zeros((ITERS - 1 - column,), jnp.float32)
        columns_re.append(jnp.concatenate([dots[0], length[None], tail]))
        columns_im.append(jnp.concatenate([dots[1], jnp.zeros((1,), jnp.float32), tail]))
        directions.append(direction)
        if column + 1 < ITERS:
            basis.append(image / length)
    hessenberg = jnp.stack([jnp.stack(columns_re, 1), jnp.stack(columns_im, 1)])
    solved = least_squares(hessenberg, beta)
    solution = jnp.zeros_like(right_side)
    for column in range(ITERS):
        solution = solution + complex_scale(
            solved[column], solved[ITERS + column], directions[column]
        )
    return (solution, hessenberg)


def solution(mesh):
    finer = Mesh(mesh.devices.reshape(2, 4, 2, 4, 4), ("gx_0", "gx_1", "gx_2", "gy_0", "gy_1"))
    in_specs = (
        P(None, GX, GY, None),
        P(GX, GY, None),
        P(GX, GY, None),
        P(GX, GY, None),
        P(None, GX_GY, None),
    )
    out_specs = (P(None, GX, GY, None), P())
    return jax.shard_map(body, mesh=finer, in_specs=in_specs, out_specs=out_specs, check_vma=False)
```

profile of v0, /device:TPU:1, one launch (start us, length us, event | category | flops | bytes accessed | tf_op | source)
XLA Modules:
  0.0 840.7 jit_solution(16100116603468770971)
XLA Ops:
  2.5 10.6 %psum.315 = f32[]{:T(128)} all-reduce(f32[]{:T(128)} %multiply_reduce_fusion.3), channel_id=1, replica_groups=mesh['gx_0'=2,'gx_1'=4,'gx_2'=2,'gy_0'=4,'gy_1'=4] {'gx_0'}, use_global_device_ids=true, to_apply=%region_1.0 | all-reduce | flops 1 | bytes 8 | tf_op jit(solution)/shard_map/psum | solution.py:88
  28.5 9.3 %psum.318 = f32[]{:T(128)} all-reduce(f32[]{:T(128)} %psum.317), channel_id=1, replica_groups=mesh['gx_0'=2,'gx_1'=4,'gx_2'=2,'gy_0'=4,'gy_1'=4] {'gy_0'}, use_global_device_ids=true, to_apply=%region_4.0 | all-reduce | flops 1 | bytes 8 | tf_op jit(solution)/shard_map/psum | solution.py:88
  37.8 10.3 %psum.319 = f32[]{:T(128)} all-reduce(f32[]{:T(128)} %psum.318), channel_id=1, replica_groups=mesh['gx_0'=2,'gx_1'=4,'gx_2'=2,'gy_0'=4,'gy_1'=4] {'gy_1'}, use_global_device_ids=true, to_apply=%region_5.0 | all-reduce | flops 1 | bytes 8 | tf_op jit(solution)/shard_map/psum | solution.py:88
  84.3 15.5 %all-gather.20 = f32[4,2,16]{2,1,0:T(2,128)S(1)} all-gather(f32[1,2,16]{2,1,0:T(2,128)S(1)} %bitcast.1144), channel_id=2, replica_groups=mesh['gx_0'=2,'gx_1'=4,'gx_2'=2,'gy_0'=4,'gy_1'=4] {'gy_1'}, dimensions={0}, use_global_device_ids=true | all-gather | bytes 640 | tf_op jit(solution)/shard_map/all_gather | solution.py:31
  115.7 16.0 %all-gather.3 = f32[8,4,4,2,16]{4,2,3,1,0:T(4,128)S(1)} all-gather(f32[2,4,4,2,16]{4,2,3,1,0:T(4,128)S(1)} %bitcast.1135), channel_id=5, replica_groups=mesh['gx_0'=2,'gx_1'=4,'gx_2'=2,'gy_0'=4,'gy_1'=4] {'gx_1'}, dimensions={0}, use_global_device_ids=true | all-gather | bytes 20480 | tf_op jit(solution)/shard_map/all_gather | solution.py:31
  131.6 16.2 %all-gather.4 = f32[8,2,4,4,2,16]{5,3,4,2,1,0:T(4,128)S(1)} all-gather(f32[4,2,4,4,2,16]{5,3,4,2,1,0:T(4,128)S(1)} %bitcast.1130), channel_id=6, replica_groups=mesh['gx_0'=2,'gx_1'=4,'gx_2'=2,'gy_0'=4,'gy_1'=4] {'gx_0'}, dimensions={0}, use_global_device_ids=true | all-gather | bytes 49152 | tf_op jit(solution)/shard_map/all_gather | solution.py:31
  184.7 14.2 %all-reduce.45 = (f32[2,1]{0,1:T(1,128)S(1)}, f32[]{:T(128)}) all-reduce(f32[2,1]{0,1:T(1,128)S(1)} %get-tuple-element.1070, f32[]{:T(128)} %get-tuple-element.1071), channel_id=1, replica_groups=mesh['gx_0'=2,'gx_1'=4,'gx_2'=2,'gy_0'=4,'gy_1'=4] {'gx_1'}, use_global_device_ids=true, to_apply=%region_13.14 | all-reduce | flops 3 | bytes 24 | tf_op jit(solution)/shard_map/psum | solution.py:88
  201.9 10.6 %all-reduce.41 = (f32[2,1]{0,1:T(1,128)S(1)}, f32[]{:T(128)}) all-reduce(f32[2,1]{0,1:T(1,128)S(1)} %get-tuple-element.1062, f32[]{:T(128)} %get-tuple-element.1063), channel_id=1, replica_groups=mesh['gx_0'=2,'gx_1'=4,'gx_2'=2,'gy_0'=4,'gy_1'=4] {'gy_0'}, use_global_device_ids=true, to_apply=%region_15.16 | all-reduce | flops 3 | bytes 24 | tf_op jit(solution)/shard_map/psum | solution.py:88
  260.4 9.8 %all-gather.21 = f32[4,2,16]{2,1,0:T(2,128)S(1)} all-gather(f32[1,2,16]{2,1,0:T(2,128)S(1)} %bitcast.1146), channel_id=7, replica_groups=mesh['gx_0'=2,'gx_1'=4,'gx_2'=2,'gy_0'=4,'gy_1'=4] {'gy_1'}, dimensions={0}, use_global_device_ids=true | all-gather | bytes 640 | tf_op jit(solution)/shard_map/all_gather | solution.py:31
  284.7 14.0 %all-gather.8 = f32[8,4,4,2,16]{4,2,3,1,0:T(4,128)S(1)} all-gather(f32[2,4,4,2,16]{4,2,3,1,0:T(4,128)S(1)} %bitcast.1136), channel_id=10, replica_groups=mesh['gx_0'=2,'gx_1'=4,'gx_2'=2,'gy_0'=4,'gy_1'=4] {'gx_1'}, dimensions={0}, use_global_device_ids=true | all-gather | bytes 20480 | tf_op jit(solution)/shard_map/all_gather | solution.py:31
  298.7 10.2 %all-gather.9 = f32[8,2,4,4,2,16]{5,3,4,2,1,0:T(4,128)S(1)} all-gather(f32[4,2,4,4,2,16]{5,3,4,2,1,0:T(4,128)S(1)} %bitcast.1131), channel_id=11, replica_groups=mesh['gx_0'=2,'gx_1'=4,'gx_2'=2,'gy_0'=4,'gy_1'=4] {'gx_0'}, dimensions={0}, use_global_device_ids=true | all-gather | bytes 49152 | tf_op jit(solution)/shard_map/all_gather | solution.py:31
  346.6 13.9 %all-reduce.44 = (f32[2,2]{0,1:T(2,128)S(1)}, f32[]{:T(128)}) all-reduce(f32[2,2]{0,1:T(2,128)S(1)} %get-tuple-element.1068, f32[]{:T(128)} %get-tuple-element.1069), channel_id=1, replica_groups=mesh['gx_0'=2,'gx_1'=4,'gx_2'=2,'gy_0'=4,'gy_1'=4] {'gx_1'}, use_global_device_ids=true, to_apply=%region_33.34 | all-reduce | flops 5 | bytes 40 | tf_op jit(solution)/shard_map/psum | solution.py:88
  363.6 10.6 %all-reduce.40 = (f32[2,2]{0,1:T(2,128)S(1)}, f32[]{:T(128)}) all-reduce(f32[2,2]{0,1:T(2,128)S(1)} %get-tuple-element.1060, f32[]{:T(128)} %get-tuple-element.1061), channel_id=1, replica_groups=mesh['gx_0'=2,'gx_1'=4,'gx_2'=2,'gy_0'=4,'gy_1'=4] {'gy_0'}, use_global_device_ids=true, to_apply=%region_35.36 | all-reduce | flops 5 | bytes 40 | tf_op jit(solution)/shard_map/psum | solution.py:88
  416.0 9.3 %while.119 = (s32[]{:T(128)}, f32[2,16]{1,0:T(2,128)S(1)}, f32[2,65536]{1,0:T(2,128)}, s32[65536]{0:T(1024)S(1)}, s32[]{:T(128)}, /*index=5*/s32[]{:T(128)}, s32[]{:T(128)}, s32[]{:T(128)}) while((s32[]{:T(128)}, f32[2,16]{1,0:T(2,128)S(1)}, f32[2,65536]{1,0:T(2,128)}, s32[65536]{0:T(1024)S(1)}, s32[]{:T(128)}, ...), condition=%wide.region_45.46_spmd.clone, body=%wide.region_44.45_spmd.clone.sunk | while | flops 6553671 | bytes 328085 | solution.py:183
  425.3 9.9 %all-gather.22 = f32[4,2,16]{2,1,0:T(2,128)S(1)} all-gather(f32[1,2,16]{2,1,0:T(2,128)S(1)} %bitcast.1145), channel_id=12, replica_groups=mesh['gx_0'=2,'gx_1'=4,'gx_2'=2,'gy_0'=4,'gy_1'=4] {'gy_1'}, dimensions={0}, use_global_device_ids=true | all-gather | bytes 640 | tf_op jit(solution)/shard_map/all_gather | solution.py:31
  450.4 15.1 %all-gather.13 = f32[8,4,4,2,16]{4,2,3,1,0:T(4,128)S(1)} all-gather(f32[2,4,4,2,16]{4,2,3,1,0:T(4,128)S(1)} %bitcast.1137), channel_id=15, replica_groups=mesh['gx_0'=2,'gx_1'=4,'gx_2'=2,'gy_0'=4,'gy_1'=4] {'gx_1'}, dimensions={0}, use_global_device_ids=true | all-gather | bytes 20480 | tf_op jit(solution)/shard_map/all_gather | solution.py:31
  465.5 10.2 %all-gather.14 = f32[8,2,4,4,2,16]{5,3,4,2,1,0:T(4,128)S(1)} all-gather(f32[4,2,4,4,2,16]{5,3,4,2,1,0:T(4,128)S(1)} %bitcast.1132), channel_id=16, replica_groups=mesh['gx_0'=2,'gx_1'=4,'gx_2'=2,'gy_0'=4,'gy_1'=4] {'gx_0'}, dimensions={0}, use_global_device_ids=true | all-gather | bytes 49152 | tf_op jit(solution)/shard_map/all_gather | solution.py:31
  515.8 13.8 %all-reduce.43 = (f32[2,3]{0,1:T(4,128)S(1)}, f32[]{:T(128)}) all-reduce(f32[2,3]{0,1:T(4,128)S(1)} %get-tuple-element.1066, f32[]{:T(128)} %get-tuple-element.1067), channel_id=1, replica_groups=mesh['gx_0'=2,'gx_1'=4,'gx_2'=2,'gy_0'=4,'gy_1'=4] {'gx_1'}, use_global_device_ids=true, to_apply=%region_55.56 | all-reduce | flops 7 | bytes 56 | tf_op jit(solution)/shard_map/psum | solution.py:88
  532.8 10.4 %all-reduce.39 = (f32[2,3]{0,1:T(4,128)S(1)}, f32[]{:T(128)}) all-reduce(f32[2,3]{0,1:T(4,128)S(1)} %get-tuple-element.1058, f32[]{:T(128)} %get-tuple-element.1059), channel_id=1, replica_groups=mesh['gx_0'=2,'gx_1'=4,'gx_2'=2,'gy_0'=4,'gy_1'=4] {'gy_0'}, use_global_device_ids=true, to_apply=%region_57.58 | all-reduce | flops 7 | bytes 56 | tf_op jit(solution)/shard_map/psum | solution.py:88
  590.8 9.8 %all-gather.23 = f32[4,2,16]{2,1,0:T(2,128)S(1)} all-gather(f32[1,2,16]{2,1,0:T(2,128)S(1)} %bitcast.1143), channel_id=17, replica_groups=mesh['gx_0'=2,'gx_1'=4,'gx_2'=2,'gy_0'=4,'gy_1'=4] {'gy_1'}, dimensions={0}, use_global_device_ids=true | all-gather | bytes 640 | tf_op jit(solution)/shard_map/all_gather | solution.py:31
  615.7 14.9 %all-gather.18 = f32[8,4,4,2,16]{4,2,3,1,0:T(4,128)S(1)} all-gather(f32[2,4,4,2,16]{4,2,3,1,0:T(4,128)S(1)} %bitcast.1138), channel_id=20, replica_groups=mesh['gx_0'=2,'gx_1'=4,'gx_2'=2,'gy_0'=4,'gy_1'=4] {'gx_1'}, dimensions={0}, use_global_device_ids=true | all-gather | bytes 20480 | tf_op jit(solution)/shard_map/all_gather | solution.py:31
  630.6 10.3 %all-gather.19 = f32[8,2,4,4,2,16]{5,3,4,2,1,0:T(4,128)S(1)} all-gather(f32[4,2,4,4,2,16]{5,3,4,2,1,0:T(4,128)S(1)} %bitcast.1133), channel_id=21, replica_groups=mesh['gx_0'=2,'gx_1'=4,'gx_2'=2,'gy_0'=4,'gy_1'=4] {'gx_0'}, dimensions={0}, use_global_device_ids=true | all-gather | bytes 49152 | tf_op jit(solution)/shard_map/all_gather | solution.py:31
  675.2 14.0 %all-reduce.42 = (f32[2,4]{0,1:T(4,128)S(1)}, f32[]{:T(128)}) all-reduce(f32[2,4]{0,1:T(4,128)S(1)} %get-tuple-element.1064, f32[]{:T(128)} %get-tuple-element.1065), channel_id=1, replica_groups=mesh['gx_0'=2,'gx_1'=4,'gx_2'=2,'gy_0'=4,'gy_1'=4] {'gx_1'}, use_global_device_ids=true, to_apply=%region_79.80 | all-reduce | flops 9 | bytes 72 | tf_op jit(solution)/shard_map/psum | solution.py:88
  692.3 10.1 %all-reduce.38 = (f32[2,4]{0,1:T(4,128)S(1)}, f32[]{:T(128)}) all-reduce(f32[2,4]{0,1:T(4,128)S(1)} %get-tuple-element.1056, f32[]{:T(128)} %get-tuple-element.1057), channel_id=1, replica_groups=mesh['gx_0'=2,'gx_1'=4,'gx_2'=2,'gy_0'=4,'gy_1'=4] {'gy_0'}, use_global_device_ids=true, to_apply=%region_81.82 | all-reduce | flops 9 | bytes 72 | tf_op jit(solution)/shard_map/psum | solution.py:88
  (545 shorter events, 539.9 us)
Async XLA Ops:
  50.0 13.1 %collective-permute-start.4 = (f32[2,2,32,128]{3,2,1,0:T(8,128)S(1)}, f32[2,2,32,128]{3,2,1,0:T(8,128)S(1)}, u32[]{:S(2)}, u32[]{:S(2)}) collective-permute-start(f32[2,2,32,128]{3,2,1,0:T(8,128)S(1)} %get-tuple-element.1250), channel_id=1, source_target_pairs={{0,16},{16,32},{32,48},{48,64},{64,80},{80,96},{96,112},{112,128},... | collective-permute-start | bytes 196616 | tf_op jit(solution)/shard_map/ppermute | solution.py:79
  55.5 7.6 collective-permute-start.5
  57.7 8.1 collective-permute-start
  61.2 5.9 collective-permute-start.1
  63.2 8.0 collective-permute-start.6
  64.5 6.7 collective-permute-start.7
  158.8 13.5 %collective-permute-start.8 = (f32[2,1,32,128]{3,2,1,0:T(8,128)S(1)}, f32[2,1,32,128]{3,2,1,0:T(8,128)S(1)}, u32[]{:S(2)}, u32[]{:S(2)}) collective-permute-start(f32[2,1,32,128]{3,2,1,0:T(8,128)S(1)} %get-tuple-element.1249), channel_id=1, source_target_pairs={{16,0},{32,16},{48,32},{64,48},{80,64},{96,80},{112,96},{128,112},... | collective-permute-start | bytes 98312 | tf_op jit(solution)/shard_map/ppermute | solution.py:63
  164.2 8.1 collective-permute-start.9
  166.1 5.5 collective-permute-start.10
  224.0 7.1 collective-permute-start.12
  229.2 5.6 collective-permute-start.13
  319.8 13.7 %collective-permute-start.16 = (f32[2,1,32,128]{3,2,1,0:T(8,128)S(1)}, f32[2,1,32,128]{3,2,1,0:T(8,128)S(1)}, u32[]{:S(2)}, u32[]{:S(2)}) collective-permute-start(f32[2,1,32,128]{3,2,1,0:T(8,128)S(1)} %get-tuple-element.1239), channel_id=1, source_target_pairs={{16,0},{32,16},{48,32},{64,48},{80,64},{96,80},{112,96},{128,112},... | collective-permute-start | bytes 98312 | tf_op jit(solution)/shard_map/ppermute | solution.py:63
  325.2 8.3 collective-permute-start.17
  327.4 5.5 collective-permute-start.18
  388.3 7.1 collective-permute-start.20
  393.1 5.6 collective-permute-start.21
  486.7 13.8 %collective-permute-start.24 = (f32[2,1,32,128]{3,2,1,0:T(8,128)S(1)}, f32[2,1,32,128]{3,2,1,0:T(8,128)S(1)}, u32[]{:S(2)}, u32[]{:S(2)}) collective-permute-start(f32[2,1,32,128]{3,2,1,0:T(8,128)S(1)} %get-tuple-element.1227), channel_id=1, source_target_pairs={{16,0},{32,16},{48,32},{64,48},{80,64},{96,80},{112,96},{128,112},... | collective-permute-start | bytes 98312 | tf_op jit(solution)/shard_map/ppermute | solution.py:63
  492.1 8.4 collective-permute-start.25
  494.3 5.5 collective-permute-start.26
  557.1 7.5 collective-permute-start.28
  562.3 5.6 collective-permute-start.29
  645.3 13.7 %collective-permute-start.32 = (f32[2,1,32,128]{3,2,1,0:T(8,128)S(1)}, f32[2,1,32,128]{3,2,1,0:T(8,128)S(1)}, u32[]{:S(2)}, u32[]{:S(2)}) collective-permute-start(f32[2,1,32,128]{3,2,1,0:T(8,128)S(1)} %get-tuple-element.1213), channel_id=1, source_target_pairs={{16,0},{32,16},{48,32},{64,48},{80,64},{96,80},{112,96},{128,112},... | collective-permute-start | bytes 98312 | tf_op jit(solution)/shard_map/ppermute | solution.py:63
  650.7 8.3 collective-permute-start.33
  652.8 5.5 collective-permute-start.34
  (81 other events, 1169.2 us)
where the time goes:
time: 855 us; the launch traced here: 841 us
  blocking collectives  430 us (50%)
  other arithmetic  137 us (16%)
  starting transfers between devices  107 us (13%)
  between operations  55 us (6%)
  matrix products  44.4 us (5%)
  local copies, waits for them, and re-layouts  39.5 us (5%)
  waiting for transfers between devices  27.2 us (3%)
    psum x25, blocking collectives, by_axis(): return functools.reduce(lax.psum, axes, x)  217 us
    all_gather x20, blocking collectives, stacked_from(): pieces = lax.all_gather(pieces, axes[k])  213 us
    reduce_sum x34, other arithmetic, least_squares(): weight = jnp.sum(ortho[position] * vector)  64.5 us
    ppermute x10, starting transfers between devices, with_halo_2(): lax.ppermute(lax.slice_in_dim(block, block.shape[dim] - width, None, axis...  38.9 us
    ppermute x8, starting transfers between devices, with_halo(): lax.ppermute(first, axis, [(b, a) for a, b in up])  26.7 us
    ppermute x10, waiting for transfers between devices, with_halo_2(): lax.ppermute(lax.slice_in_dim(block, 0, width, axis=dim), axis, backward)  24.6 us
    ppermute x8, starting transfers between devices, with_halo(): lax.ppermute(last, axis, up)  24.4 us
    dot_general x16, matrix products, accumulate(): lax.dot_general(piece, onehot, (((1,), (1,)), ((), ())), precision=lax.Pr...  23.3 us
  transfers between devices with their start and end apart: 36, of which 12 were waited for; matrix products, arithmetic and copies ran while one was open for 0% of the time, Pallas kernels for 0%

commit v1 on v0

v1 whole, which is shorter than its diff:
```python
import functools

import jax
import jax.numpy as jnp
from jax import lax
from jax.experimental import pallas as pl
from jax.experimental.pallas import tpu as pltpu
from jax.sharding import Mesh
from jax.sharding import PartitionSpec as P

ITERS = 4
AXES = ("zh", "px", "co", "py", "zl")
GX = ("zh", "px", "co")
GY = ("py", "zl")
damping = 0.8
pml_strength = 3.0
epsilon = 1e-06

FRONT = 8
PITCH = 40
HALO = 3
NXD = 16
NYD = 32
ROWS = FRONT + (NXD + 2 * HALO) * PITCH
MESH = pl.DeviceIdType.MESH
DIRS = [(-1, -1), (-1, 0), (-1, 1), (0, -1), (0, 1), (1, -1), (1, 0), (1, 1)]
CORNERS = [(-1, -1), (-1, 1), (1, -1), (1, 1)]
F32 = jnp.float32


def row_of(e, t=0):
    return FRONT + e * PITCH + t * 8


def kernel(
    rhs, wave, layer, agg, cinv,
    sol, hess,
    wv, lf, ag, dg, ab, sr, si, idx,
    z, u, m, v, f, p, rem,
    dre, dim, g1, g2, cown, crecv,
    iy_s, iy_r, ic_s, ic_r, uy_s, uy_r, uc_s, uc_r,
    sem_s, sem_r,
):
    zh, px, co = lax.axis_index("zh"), lax.axis_index("px"), lax.axis_index("co")
    py, zl = lax.axis_index("py"), lax.axis_index("zl")
    gx = zh * 8 + px * 2 + co
    gy = py * 4 + zl
    s1 = (zh * 2 + co) * 4 + zl
    s2 = px * 4 + py

    def device(a, b):
        return (
            lax.div(a, 8), lax.rem(lax.div(a, 2), 4), lax.rem(a, 2), lax.div(b, 4), lax.rem(b, 4)
        )

    def beside_device(dx, dy):
        return device(lax.rem(gx + 16 + dx, 16), lax.rem(gy + 16 + dy, 16))

    def member1(k):
        s = lax.rem(s1 + k, 16)
        return (lax.div(s, 8), px, lax.rem(lax.div(s, 4), 2), py, lax.rem(s, 4))

    def member2(k):
        s = lax.rem(s2 + k, 16)
        return (zh, lax.div(s, 4), co, lax.rem(s, 4), zl)

    lane = lax.broadcasted_iota(jnp.int32, (8, 128), 1)
    sub = lax.broadcasted_iota(jnp.int32, (8, 128), 0)
    lane1 = lax.broadcasted_iota(jnp.int32, (1, 128), 1)
    zero = jnp.zeros((8, 128), F32)

    barrier = pltpu.get_barrier_semaphore()
    for dx, dy in DIRS:
        pl.semaphore_signal(barrier, inc=1, device_id=beside_device(dx, dy), device_id_type=MESH)

    def greet(k, carry):
        pl.semaphore_signal(barrier, inc=1, device_id=member1(k), device_id_type=MESH)
        pl.semaphore_signal(barrier, inc=1, device_id=member2(k), device_id_type=MESH)
        return carry

    lax.fori_loop(1, 16, greet, 0)

    def send(src, dst, kind, target):
        pltpu.make_async_remote_copy(
            src_ref=src,
            dst_ref=dst,
            send_sem=sem_s.at[kind],
            recv_sem=sem_r.at[kind],
            device_id=target,
            device_id_type=MESH,
        ).start()

    def take(like, sem):
        pltpu.make_async_copy(like, like, sem).wait()

    def coefficients(w, lay):
        wave_sq = w * w
        depth = lay / 3.0
        absorb = wave_sq * (pml_strength * depth * depth)
        diag = 6.0 - wave_sq
        magnitude = diag * diag + absorb * absorb
        return diag, absorb, damping * diag / magnitude, damping * absorb / magnitude

    def own_rows(x, carry):
        for t in range(4):
            here = pl.ds(pl.multiple_of(row_of(x + HALO, t), 8), 8)
            there = pl.ds(8 * t, 8)
            w = wave[x, there, :]
            lay = layer[x, there, :].astype(F32)
            which = agg[x, there, :]
            wv[here, :] = w
            lf[here, :] = lay
            ag[here, :] = which.astype(F32)
            idx[here, :] = which
            d, a, r, i = coefficients(w, lay)
            dg[here, :] = d
            ab[here, :] = a
            sr[here, :] = r
            si[here, :] = i
            z[0, 0, here, :] = rhs[0, x, there, :]
            z[0, 1, here, :] = rhs[1, x, there, :]
        return carry

    lax.fori_loop(0, NXD, own_rows, 0)

    def clear(k, carry):
        ag[pl.ds(pl.multiple_of(k * PITCH, 8), 8), :] = zero
        return carry

    lax.fori_loop(0, NXD + 2 * HALO + 1, clear, 0)

    def y_columns(ref, y):
        return ref[pl.ds(row_of(HALO) + y, NXD, stride=PITCH), :]

    def pack_y(buf, fields):
        at = 0
        for ref, width in fields:
            for s in range(width):
                buf[0, at] = y_columns(ref, s)
                buf[1, at] = y_columns(ref, NYD - width + s)
                at += 1

    def unpack_y(buf, fields):
        at = 0
        for ref, width in fields:
            for s in range(width):
                ref[pl.ds(row_of(HALO) + NYD + s, NXD, stride=PITCH), :] = buf[0, at]
                ref[pl.ds(row_of(HALO) - width + s, NXD, stride=PITCH), :] = buf[1, at]
                at += 1

    def send_x(fields, kind):
        for ref, width in fields:
            for s in range(width):
                low = pl.ds(row_of(HALO + s), NYD)
                high = pl.ds(row_of(HALO + NXD - width + s), NYD)
                past = pl.ds(row_of(HALO + NXD + s), NYD)
                ahead = pl.ds(row_of(HALO - width + s), NYD)
                send(ref.at[low], ref.at[past], kind, beside_device(-1, 0))
                send(ref.at[high], ref.at[ahead], kind, beside_device(1, 0))

    def send_y(out, into, kind):
        send(out.at[0], into.at[0], kind, beside_device(0, -1))
        send(out.at[1], into.at[1], kind, beside_device(0, 1))

    def edge_row(dx, dy, ox, oy):
        x = ox if dx < 0 else NXD - 1 - ox
        y = oy if dy < 0 else NYD - 1 - oy
        return row_of(HALO + x) + y

    def past_row(dx, dy, ox, oy):
        x = -1 - ox if dx < 0 else NXD + ox
        y = -1 - oy if dy < 0 else NYD + oy
        return row_of(HALO + x) + y

    def pack_corners(buf, cells):
        for k, (dx, dy) in enumerate(CORNERS):
            for at, (ref, ox, oy) in enumerate(cells):
                buf[k, pl.ds(at, 1), :] = ref[pl.ds(edge_row(dx, dy, ox, oy), 1), :]

    def send_corners(out, into, kind):
        for k, (dx, dy) in enumerate(CORNERS):
            send(out.at[k], into.at[3 - k], kind, beside_device(dx, dy))

    def unpack_corners(buf, cells):
        for k, (dx, dy) in enumerate(CORNERS):
            for at, (ref, ox, oy) in enumerate(cells):
                ref[pl.ds(past_row(dx, dy, ox, oy), 1), :] = buf[k, pl.ds(at, 1), :]

    first_fields = [(z.at[0, 0], 2), (z.at[0, 1], 2), (wv, 2), (lf, 2), (ag, 3)]
    first_cells = [(ref, 0, 0) for ref, _ in first_fields] + [(ag, 1, 0), (ag, 0, 1)]
    pack_y(iy_s, first_fields)
    pack_corners(ic_s, first_cells)

    pl.semaphore_wait(barrier, len(DIRS) + 30)

    send_x(first_fields, 0)
    send_y(iy_s, iy_r, 1)
    send_corners(ic_s, ic_r, 2)

    lane16 = lax.broadcasted_iota(jnp.int32, (16, 128), 1)
    low16 = lane16 < 64

    def arrange(a, carry):
        at_a = lax.rem(lax.div(a, 2), 4) * 16 + lax.div(a, 8) * 2 + lax.rem(a, 2)
        for half in range(2):
            cols = pl.ds(pl.multiple_of(a * 256 + half * 128, 128), 128)
            c_re, c_im = cinv[0, :, cols], cinv[1, :, cols]
            r_re, r_im = pltpu.roll(c_re, 64, axis=1), pltpu.roll(c_im, 64, axis=1)
            at = at_a + (2 * half) * 4
            dre[at] = jnp.where(low16, c_re, -r_im)
            dim[at] = jnp.where(low16, c_im, r_re)
            dre[at + 4] = jnp.where(low16, r_re, -c_im)
            dim[at + 4] = jnp.where(low16, r_im, c_re)
        return carry

    lax.fori_loop(0, 16, arrange, 0)

    take(u.at[0, 0, pl.ds(0, 22 * NYD)], sem_r.at[0])
    take(iy_r, sem_r.at[1])
    take(ic_r, sem_r.at[2])
    unpack_y(iy_r, first_fields)
    unpack_corners(ic_r, first_cells)

    def x_inside(e):
        below = jnp.where(gx > 0, 1, 0)
        above = jnp.where(gx < 15, 1, 0)
        return jnp.where(e < HALO, below, jnp.where(e >= HALO + NXD, above, 1))

    y_up = jnp.where(gy < 15, 1, 0)
    y_down = jnp.where(gy > 0, 1, 0)

    def halo_tile(e, t, with_coefficients):
        here = pl.ds(pl.multiple_of(row_of(e, t), 8), 8)
        if t < 4:
            inside = jnp.full((8, 128), x_inside(e), jnp.int32) > 0
        else:
            inside = jnp.where(sub < 4, x_inside(e) * y_up, x_inside(e + 1) * y_down) > 0
        idx[here, :] = jnp.where(inside, ag[here, :].astype(jnp.int32), 32)
        if with_coefficients:
            d, a, r, i = coefficients(wv[here, :], lf[here, :])
            dg[here, :] = d
            ab[here, :] = a
            sr[here, :] = jnp.where(inside, r, 0.0)
            si[here, :] = jnp.where(inside, i, 0.0)

    def y_halos(e, carry):
        halo_tile(e, 4, True)
        return carry

    halo_tile(-1, 4, False)
    lax.fori_loop(0, 21, y_halos, 0)
    halo_tile(21, 4, False)
    for low_e in (0, 19):

        def x_halos(k, carry):
            for t in range(4):
                halo_tile(low_e + k, t, True)
            return carry

        if low_e == 0:
            for t in range(4):
                halo_tile(0, t, False)
            lax.fori_loop(1, 3, x_halos, 0)
        else:
            lax.fori_loop(0, 2, x_halos, 0)
            for t in range(4):
                halo_tile(21, t, False)

    def neighbours(ref, c, base):
        centre = ref[c, pl.ds(base, 8), :]
        total = (
            ref[c, pl.ds(base + 1, 8), :]
            + ref[c, pl.ds(base - 1, 8), :]
            + ref[c, pl.ds(base + PITCH, 8), :]
            + ref[c, pl.ds(base - PITCH, 8), :]
        )
        up = jnp.where(lane == 127, 0.0, pltpu.roll(centre, 127, axis=1))
        down = jnp.where(lane == 0, 0.0, pltpu.roll(centre, 1, axis=1))
        return centre, total + up + down

    def operate(ref, base):
        c0, b0 = neighbours(ref, 0, base)
        c1, b1 = neighbours(ref, 1, base)
        here = pl.ds(base, 8)
        d, a = dg[here, :], ab[here, :]
        return c0, c1, d * c0 - b0 + a * c1, d * c1 - b1 - a * c0

    def over_tiles(width, body):
        low = HALO - width
        body(row_of(low - 1, 4))

        def rows(e, carry):
            for t in range(5):
                body(pl.multiple_of(row_of(e, t), 8))
            return carry

        lax.fori_loop(low, HALO + NXD + width, rows, 0)

    def smooth_all(j):
        zj, mj, uj = z.at[j], m.at[j], u.at[j]

        def make_first(base):
            here = pl.ds(base, 8)
            r, i = sr[here, :], si[here, :]
            a, b = zj[0, here, :], zj[1, here, :]
            f[0, here, :] = r * a - i * b
            f[1, here, :] = r * b + i * a

        over_tiles(2, make_first)

        def make_second(base):
            here = pl.ds(base, 8)
            f0, f1, w0, w1 = operate(f, base)
            r, i = sr[here, :], si[here, :]
            a, b = zj[0, here, :] - w0, zj[1, here, :] - w1
            mj[0, here, :] = f0 + (r * a - i * b)
            mj[1, here, :] = f1 + (r * b + i * a)

        over_tiles(1, make_second)

        def make_rest(x, carry):
            for t in range(4):
                base = pl.multiple_of(row_of(x + HALO, t), 8)
                here = pl.ds(base, 8)
                _, _, w0, w1 = operate(mj, base)
                uj[0, here, :] = w0
                uj[1, here, :] = w1
                rem[0, x, pl.ds(8 * t, 8), :] = zj[0, here, :] - w0
                rem[1, x, pl.ds(8 * t, 8), :] = zj[1, here, :] - w1
            return carry

        lax.fori_loop(0, NXD, make_rest, 0)

    def restrict():
        def rows(x, sums):
            sums = list(sums)
            for t in range(4):
                which = idx[pl.ds(pl.multiple_of(row_of(x + HALO, t), 8), 8), :]
                a, b = rem[0, x, pl.ds(8 * t, 8), :], rem[1, x, pl.ds(8 * t, 8), :]
                for g in range(16):
                    mask = which == g
                    sums[g] = sums[g] + jnp.where(mask, a, 0.0)
                    sums[16 + g] = sums[16 + g] + jnp.where(mask, b, 0.0)
            return tuple(sums)

        sums = lax.fori_loop(0, NXD, rows, (zero,) * 32)
        out = zero
        for k in range(32):
            place = (k // 16) * 64 + k % 16
            out = out + jnp.where(
                lane == zl * 16 + place, jnp.sum(sums[k], axis=1, keepdims=True), 0.0
            )
        return jnp.sum(out, axis=0, keepdims=True)

    def products(j):
        def rows(x, sums):
            sums = list(sums)
            for t in range(4):
                here = pl.ds(pl.multiple_of(row_of(x + HALO, t), 8), 8)
                a, b = z[j, 0, here, :], z[j, 1, here, :]
                sums[0] = sums[0] + (a * a + b * b)
                for i in range(j):
                    c, d = v[i, 0, here, :], v[i, 1, here, :]
                    sums[1 + 2 * i] = sums[1 + 2 * i] + (c * a + d * b)
                    sums[2 + 2 * i] = sums[2 + 2 * i] + (c * b - d * a)
            return tuple(sums)

        sums = lax.fori_loop(0, NXD, rows, (zero,) * (1 + 2 * j))
        out = zero
        for k, total in enumerate(sums):
            out = out + jnp.where(lane == k, jnp.sum(total, axis=1, keepdims=True), 0.0)
        return jnp.sum(out, axis=0, keepdims=True)

    S1, S2, CX, UX, UY, UC = 3, 8, 13, 17, 21, 25

    def start_gather(j, coarse, dots):
        mine = g1.at[j, pl.ds(2 * s1, 2)]
        g1[j, 2 * s1] = coarse if coarse is not None else jnp.zeros((1, 128), F32)
        g1[j, 2 * s1 + 1] = dots

        def step(k, carry):
            send(mine, mine, S1 + j, member1(k))
            return carry

        lax.fori_loop(1, 16, step, 0)

    def middle_gather(j):
        take(g1.at[j, pl.ds(0, 30)], sem_r.at[S1 + j])
        for q in range(4):
            g2[j, 5 * s2 + q] = (g1[j, 8 * q] + g1[j, 8 * q + 2]) + (
                g1[j, 8 * q + 4] + g1[j, 8 * q + 6]
            )
        total = g1[j, 1]
        for s in range(1, 16):
            total = total + g1[j, 2 * s + 1]
        g2[j, 5 * s2 + 4] = total
        mine = g2.at[j, pl.ds(5 * s2, 5)]

        def step(k, carry):
            send(mine, mine, S2 + j, member2(k))
            return carry

        lax.fori_loop(1, 16, step, 0)

    def end_gather(j):
        take(g2.at[j, pl.ds(0, 75)], sem_r.at[S2 + j])
        total = g2[j, 4]
        for s in range(1, 16):
            total = total + g2[j, 5 * s + 4]
        return [
            jnp.broadcast_to(
                jnp.sum(jnp.where(lane1 == k, total, 0.0), axis=1, keepdims=True), (8, 128)
            )
            for k in range(1 + 2 * j)
        ]

    sub16 = lax.broadcasted_iota(jnp.int32, (16, 128), 0)

    def coarse_solve(j):
        def step(k, sums):
            a, b = sums
            for q in range(4):
                row = g2[j, 5 * k + q]
                a = a + dre[4 * k + q] * row
                b = b + dim[4 * k + q] * row
            return a, b

        empty = jnp.zeros((16, 128), F32)
        a, b = lax.fori_loop(0, 16, step, (empty, empty))
        own = lane16 == sub16
        re = jnp.sum(
            jnp.where(own, jnp.sum(a, axis=1, keepdims=True), 0.0), axis=0, keepdims=True
        )
        im = jnp.sum(
            jnp.where(own, jnp.sum(b, axis=1, keepdims=True), 0.0), axis=0, keepdims=True
        )
        cown[j, 0] = re + pltpu.roll(jnp.broadcast_to(im, (8, 128)), 16, axis=1)[0:1]
        for k, (dx, dy) in enumerate(DIRS):
            send(cown.at[j], crecv.at[j, pl.ds(7 - k, 1)], CX + j, beside_device(dx, dy))
        return re, im

    def spread(table, here):
        which = idx[here, :]
        return (
            jnp.take_along_axis(table, which, axis=1, mode="promise_in_bounds"),
            jnp.take_along_axis(table, which + 16, axis=1, mode="promise_in_bounds"),
        )

    def prolong(j):
        take(crecv.at[j], sem_r.at[CX + j])

        def row(dx, dy):
            if (dx, dy) == (0, 0):
                return jnp.broadcast_to(cown[j, 0], (8, 128))
            return jnp.broadcast_to(crecv[j, DIRS.index((dx, dy))], (8, 128))

        def place(table, base):
            here = pl.ds(base, 8)
            a, b = spread(table, here)
            p[0, here, :] = a
            p[1, here, :] = b

        def side(e):
            return -1 if e < HALO else (1 if e >= HALO + NXD else 0)

        def halo_table(e):
            return jnp.where(sub < 4, row(side(e), 1), row(side(e + 1), -1))

        place(halo_table(-1), row_of(-1, 4))
        for e in [0, 1, 2, 18, 19, 20, 21]:
            table = row(side(e), 0)
            for t in range(4):
                place(table, row_of(e, t))
            place(halo_table(e), row_of(e, 4))
        table, edge = row(0, 0), halo_table(HALO)

        def rows(e, carry):
            for t in range(4):
                place(table, pl.multiple_of(row_of(e, t), 8))
            place(edge, pl.multiple_of(row_of(e, 4), 8))
            return carry

        lax.fori_loop(3, 18, rows, 0)

    def send_halo(j):
        fields = [(u.at[j, 0], 2), (u.at[j, 1], 2)]
        cells = [(u.at[j, 0], 0, 0), (u.at[j, 1], 0, 0)]
        pack_y(uy_s.at[j], fields)
        pack_corners(uc_s.at[j], cells)
        send_x(fields, UX + j)
        send_y(uy_s.at[j], uy_r.at[j], UY + j)
        send_corners(uc_s.at[j], uc_r.at[j], UC + j)

    def take_halo(j):
        fields = [(u.at[j, 0], 2), (u.at[j, 1], 2)]
        cells = [(u.at[j, 0], 0, 0), (u.at[j, 1], 0, 0)]
        take(z.at[4, 0, pl.ds(0, 8 * NYD)], sem_r.at[UX + j])
        take(uy_r.at[j], sem_r.at[UY + j])
        take(uc_r.at[j], sem_r.at[UC + j])
        unpack_y(uy_r.at[j], fields)
        unpack_corners(uc_r.at[j], cells)

    def over_own(body):
        def rows(x, carry):
            for t in range(4):
                body(pl.multiple_of(row_of(x + HALO, t), 8))
            return carry

        lax.fori_loop(0, NXD, rows, 0)

    columns = []
    lengths = []
    coarse = []

    def finish(j, dots):
        squared = dots[0]
        col = [(dots[1 + 2 * i], dots[2 + 2 * i]) for i in range(j)]
        for re, im in col:
            squared = squared - (re * re + im * im)
        if j > 0:
            squared = jnp.maximum(squared, 0.0)
            columns.append(col)
        lengths.append(jnp.sqrt(squared + epsilon))

    for j in range(ITERS):
        smooth_all(j)
        start_gather(j, restrict(), products(j))
        if j + 1 < ITERS:
            send_halo(j)
        middle_gather(j)
        if j + 1 < ITERS:
            take_halo(j)
        dots = end_gather(j)
        coarse.append(coarse_solve(j))
        finish(j, dots)
        inverse = 1.0 / lengths[j]
        col = columns[j - 1] if j else []

        def make_basis(base):
            here = pl.ds(base, 8)
            a, b = z[j, 0, here, :], z[j, 1, here, :]
            for i, (re, im) in enumerate(col):
                c, d = v[i, 0, here, :], v[i, 1, here, :]
                a = a - (re * c - im * d)
                b = b - (re * d + im * c)
            v[j, 0, here, :] = a * inverse
            v[j, 1, here, :] = b * inverse

        over_own(make_basis)

        def make_start(base):
            here = pl.ds(base, 8)
            a, b = u[j, 0, here, :], u[j, 1, here, :]
            for i, (re, im) in enumerate(col):
                c, d = z[i + 1, 0, here, :], z[i + 1, 1, here, :]
                a = a - (re * c - im * d)
                b = b - (re * d + im * c)
            z[j + 1, 0, here, :] = a
            z[j + 1, 1, here, :] = b

        if j + 1 < ITERS:
            over_tiles(2, make_start)
        else:
            over_own(make_start)
        prolong(j)

        def make_image(base):
            here = pl.ds(base, 8)
            _, _, w0, w1 = operate(p, base)
            z[j + 1, 0, here, :] = (z[j + 1, 0, here, :] + w0) * inverse
            z[j + 1, 1, here, :] = (z[j + 1, 1, here, :] + w1) * inverse

        if j + 1 < ITERS:
            over_tiles(2, make_image)
        else:
            over_own(make_image)

    start_gather(ITERS, None, products(ITERS))
    middle_gather(ITERS)
    finish(ITERS, end_gather(ITERS))

    def times(a, b):
        return (a[0] * b[0] - a[1] * b[1], a[0] * b[1] + a[1] * b[0])

    def conj_times(a, b):
        return (a[0] * b[0] + a[1] * b[1], a[0] * b[1] - a[1] * b[0])

    rotations, upper, diagonal = [], [], []
    target = [(lengths[0], zero)]
    for j in range(ITERS):
        col = list(columns[j])
        for k, (c, s) in enumerate(rotations):
            head, tail = col[k], col[k + 1]
            turned = conj_times(c, head)
            other = times(c, tail)
            col[k] = (turned[0] + s * tail[0], turned[1] + s * tail[1])
            col[k + 1] = (other[0] - s * head[0], other[1] - s * head[1])
        below = lengths[j + 1]
        a = col[j]
        size = jnp.sqrt(a[0] * a[0] + a[1] * a[1] + below * below)
        c, s = (a[0] / size, a[1] / size), below / size
        rotations.append((c, s))
        upper.append(col)
        diagonal.append(size)
        last = target[j]
        target[j] = conj_times(c, last)
        target.append((-s * last[0], -s * last[1]))
    solved = [None] * ITERS
    for j in reversed(range(ITERS)):
        re, im = target[j]
        for k in range(j + 1, ITERS):
            part = times(upper[k][j], solved[k])
            re, im = re - part[0], im - part[1]
        solved[j] = (re / diagonal[j], im / diagonal[j])

    weights = [None] * ITERS
    for j in reversed(range(ITERS)):
        inverse = 1.0 / lengths[j]
        weights[j] = (solved[j][0] * inverse, solved[j][1] * inverse)
        if j:
            for i, h in enumerate(columns[j - 1]):
                part = times(h, weights[j])
                solved[i] = (solved[i][0] - part[0], solved[i][1] - part[1])

    c_re, c_im = zero, zero
    for j in range(ITERS):
        wr, wi = weights[j]
        c_re = c_re + (wr * coarse[j][0] - wi * coarse[j][1])
        c_im = c_im + (wr * coarse[j][1] + wi * coarse[j][0])
    table = c_re + pltpu.roll(c_im, 16, axis=1)

    def write(x, carry):
        for t in range(4):
            here = pl.ds(pl.multiple_of(row_of(x + HALO, t), 8), 8)
            a, b = spread(table, here)
            for j in range(ITERS):
                wr, wi = weights[j]
                c, d = m[j, 0, here, :], m[j, 1, here, :]
                a = a + (wr * c - wi * d)
                b = b + (wr * d + wi * c)
            sol[0, x, pl.ds(8 * t, 8), :] = a
            sol[1, x, pl.ds(8 * t, 8), :] = b
        return carry

    lax.fori_loop(0, NXD, write, 0)

    h_re, h_im = zero, zero
    for j in range(ITERS):
        for i, (re, im) in enumerate(columns[j]):
            spot = (sub == i) & (lane == j)
            h_re = jnp.where(spot, re, h_re)
            h_im = jnp.where(spot, im, h_im)
        h_re = jnp.where((sub == j + 1) & (lane == j), lengths[j + 1], h_re)
    hess[0] = h_re
    hess[1] = h_im

    take(u.at[0, 0, pl.ds(0, 22 * NYD)], sem_s.at[0])
    take(iy_s, sem_s.at[1])
    take(ic_s, sem_s.at[2])
    for j in range(ITERS + 1):
        take(g1.at[j, pl.ds(0, 30)], sem_s.at[S1 + j])
        take(g2.at[j, pl.ds(0, 75)], sem_s.at[S2 + j])
    for j in range(ITERS):
        take(crecv.at[j], sem_s.at[CX + j])
        if j + 1 < ITERS:
            take(z.at[4, 0, pl.ds(0, 8 * NYD)], sem_s.at[UX + j])
            take(uy_s.at[j], sem_s.at[UY + j])
            take(uc_s.at[j], sem_s.at[UC + j])


def body(right_side, wavenumber, pml_layer, aggregate, coarse_inverse):
    field = pltpu.VMEM((2, ROWS, 128), F32)
    plane = pltpu.VMEM((ROWS, 128), F32)

    def fields(n):
        return pltpu.VMEM((n, 2, ROWS, 128), F32)

    vmem = pl.BlockSpec(memory_space=pltpu.VMEM)
    solution, hessenberg = pl.pallas_call(
        kernel,
        out_shape=(
            jax.ShapeDtypeStruct(right_side.shape, F32),
            jax.ShapeDtypeStruct((2, 8, 128), F32),
        ),
        in_specs=[vmem] * 5,
        out_specs=(vmem, vmem),
        scratch_shapes=[
            *[plane] * 7,
            pltpu.VMEM((ROWS, 128), jnp.int32),
            fields(5), fields(4), fields(4), fields(4),
            field, field,
            pltpu.VMEM((2, NXD, NYD, 128), F32),
            pltpu.VMEM((64, 16, 128), F32),
            pltpu.VMEM((64, 16, 128), F32),
            pltpu.VMEM((5, 32, 1, 128), F32),
            pltpu.VMEM((5, 80, 1, 128), F32),
            pltpu.VMEM((4, 1, 1, 128), F32),
            pltpu.VMEM((4, 8, 1, 128), F32),
            pltpu.VMEM((2, 11, 16, 128), F32),
            pltpu.VMEM((2, 11, 16, 128), F32),
            pltpu.VMEM((4, 8, 128), F32),
            pltpu.VMEM((4, 8, 128), F32),
            pltpu.VMEM((3, 2, 4, 16, 128), F32),
            pltpu.VMEM((3, 2, 4, 16, 128), F32),
            pltpu.VMEM((3, 4, 8, 128), F32),
            pltpu.VMEM((3, 4, 8, 128), F32),
            pltpu.SemaphoreType.DMA((28,)),
            pltpu.SemaphoreType.DMA((28,)),
        ],
        compiler_params=pltpu.CompilerParams(
            collective_id=0, has_side_effects=True, vmem_limit_bytes=60 * 1024 * 1024
        ),
    )(right_side, wavenumber, pml_layer, aggregate, coarse_inverse)
    return solution, hessenberg[:, : ITERS + 1, :ITERS]


def solution(mesh):
    finer = Mesh(mesh.devices.reshape(2, 4, 2, 4, 4), AXES)
    in_specs = (
        P(None, GX, GY, None),
        P(GX, GY, None),
        P(GX, GY, None),
        P(GX, GY, None),
        P(None, GX + GY, None),
    )
    out_specs = (P(None, GX, GY, None), P())
    return jax.shard_map(body, mesh=finer, in_specs=in_specs, out_specs=out_specs, check_vma=False)
```

time: 855 us -> 132 us (0.15); the launches traced: 841 us -> 131 us
  blocking collectives: 430 us -> 0 us
  other arithmetic: 137 us -> 0 us
  Pallas kernels: 0 us -> 128 us
  starting transfers between devices: 107 us -> 0 us
  between operations: 55 us -> 0.64 us
  matrix products: 44.4 us -> 0 us
  local copies, waits for them, and re-layouts: 39.5 us -> 3.24 us
  waiting for transfers between devices: 27.2 us -> 0 us
    psum x25 -> x0, blocking collectives: 217 us -> none  [by_axis(): return functools.reduce(lax.psum, axes, x)]
    all_gather x20 -> x0, blocking collectives: 213 us -> none  [stacked_from(): pieces = lax.all_gather(pieces, axes[k])]
    pallas_call x0 -> x1, Pallas kernels: none -> 128 us  [body(): pl.pallas_call(kernel, out_shape=(jax.ShapeDtypeStruct(right_side.shape,...]
    ppermute x36 -> x0, starting transfers between devices: 107 us -> none  [the longest x10 38.9 us: with_halo_2(): lax.ppermute(lax.slice_in_dim(block, block.shape[dim] - width, None, axis...]
    reduce_sum x57 -> x0, other arithmetic: 90.9 us -> none  [the longest x34 64.5 us: least_squares(): weight = jnp.sum(ortho[position] * vector)]
    dot_general x48 -> x0, matrix products: 44.4 us -> none  [the longest x16 23.3 us: accumulate(): lax.dot_general(piece, onehot, (((1,), (1,)), ((), ())), precision=lax.Pr...]
    ppermute x36 -> x0, waiting for transfers between devices: 27.2 us -> none  [the longest x10 24.6 us: with_halo_2(): lax.ppermute(lax.slice_in_dim(block, 0, width, axis=dim), axis, backward)]
    another operation x39 -> x0, other arithmetic: 18.4 us -> none  [the longest x13 13.4 us: body(): local_dots = jnp.stack([inner_local(member, image) for member in basis], 1)]
  transfers between devices with their start and end apart: 36 -> 0, of which waited for: 12 -> 0; matrix products, arithmetic and copies ran while one was open for 0% -> 0% of each run, Pallas kernels for 0% -> 0%
where the time goes in v1:
time: 132 us; the launch traced here: 131 us
  Pallas kernels  128 us (97%)
  local copies, waits for them, and re-layouts  3.24 us (2%)
    pallas_call x1, Pallas kernels, body(): pl.pallas_call(kernel, out_shape=(jax.ShapeDtypeStruct(right_side.shape,...  128 us
    unnamed x2, local copies, waits for them, and re-layouts  3.24 us

profile of v1, /device:TPU:1, one launch (start us, length us, event | category | flops | bytes accessed | tf_op | source)
XLA Modules:
  0.0 131.4 jit_solution(1043430300205035984)
XLA Ops:
  0.6 127.6 %shard_map.68 = (f32[2,16,32,128]{3,2,1,0:T(8,128)}, f32[2,8,128]{2,1,0:T(8,128)}) custom-call(f32[2,16,32,128]{3,2,1,0:T(8,128)} %rhs.1, f32[16,32,128]{2,1,0:T(8,128)} %wave.1, s32[16,32,128]{2,1,0:T(8,128)} %layer.1, s32[16,32,128]{2,1,0:T(8,128)} %agg.1, f32[2,16,4096]{2,1,0:T(8,128)} %cinv.1), custom_call_target="tpu_custom_call" | custom-call | tf_op jit(solution)/shard_map/pallas_call | solution.py:679
  128.2 1.4 %copy.7 = f32[2,5,4]{1,2,0:T(4,128)} copy(f32[2,5,4]{2,1,0:T(8,128)} %bitcast.1) | data formatting | bytes 320
  129.6 1.9 %copy.9 = f32[2,16,32,128]{3,2,1,0:T(8,128)} copy(f32[2,16,32,128]{3,2,1,0:T(8,128)} %get-tuple-element.10) | data formatting | bytes 1048576

commit v2 on v1

--- a/solution.py
+++ b/solution.py
@@ -28,18 +28,28 @@
 F32 = jnp.float32
 
 
+def over_rows(low, high, group, body):
+    def trip(k, carry):
+        for q in range(group):
+            body(low + k * group + q)
+        return carry
+
+    lax.fori_loop(0, (high - low) // group, trip, 0)
+
+
 def row_of(e, t=0):
     return FRONT + e * PITCH + t * 8
 
 
 def kernel(
+    rhs_in, wave_in, layer_in, agg_in, cinv_in,
+    sol, hess,
     rhs, wave, layer, agg, cinv,
-    sol, hess,
     wv, lf, ag, dg, ab, sr, si, idx,
     z, u, m, v, f, p, rem,
     dre, dim, g1, g2, cown, crecv,
     iy_s, iy_r, ic_s, ic_r, uy_s, uy_r, uc_s, uc_r,
-    sem_s, sem_r,
+    sem_s, sem_r, sem_in,
 ):
     zh, px, co = lax.axis_index("zh"), lax.axis_index("px"), lax.axis_index("co")
     py, zl = lax.axis_index("py"), lax.axis_index("zl")
@@ -56,13 +66,20 @@
     def beside_device(dx, dy):
         return device(lax.rem(gx + 16 + dx, 16), lax.rem(gy + 16 + dy, 16))
 
-    def member1(k):
-        s = lax.rem(s1 + k, 16)
-        return (lax.div(s, 8), px, lax.rem(lax.div(s, 4), 2), py, lax.rem(s, 4))
-
-    def member2(k):
-        s = lax.rem(s2 + k, 16)
-        return (zh, lax.div(s, 4), co, lax.rem(s, 4), zl)
+    far = (2, 3, 1, 0)
+    zhs = [zh, 1 - zh]
+    cos = [co, 1 - co]
+    zls = [zl] + [lax.rem(zl + k, 4) for k in range(1, 4)]
+    pxs = [px] + [lax.rem(px + k, 4) for k in range(1, 4)]
+    pys = [py] + [lax.rem(py + k, 4) for k in range(1, 4)]
+    group1 = [
+        (zhs[a], px, cos[b], py, zls[c])
+        for a in (1, 0) for c in far for b in (1, 0) if (a, b, c) != (0, 0, 0)
+    ]
+    group2 = [
+        (zh, pxs[a], co, pys[b], zl) for a in far for b in far if (a, b) != (0, 0)
+    ]
+    towards = {d: beside_device(*d) for d in DIRS}
 
     lane = lax.broadcasted_iota(jnp.int32, (8, 128), 1)
     sub = lax.broadcasted_iota(jnp.int32, (8, 128), 0)
@@ -70,15 +87,18 @@
     zero = jnp.zeros((8, 128), F32)
 
     barrier = pltpu.get_barrier_semaphore()
-    for dx, dy in DIRS:
-        pl.semaphore_signal(barrier, inc=1, device_id=beside_device(dx, dy), device_id_type=MESH)
-
-    def greet(k, carry):
-        pl.semaphore_signal(barrier, inc=1, device_id=member1(k), device_id_type=MESH)
-        pl.semaphore_signal(barrier, inc=1, device_id=member2(k), device_id_type=MESH)
-        return carry
-
-    lax.fori_loop(1, 16, greet, 0)
+    partners = group1 + group2 + list(towards.values())
+    for target in partners:
+        pl.semaphore_signal(barrier, inc=1, device_id=target, device_id_type=MESH)
+
+    loads = [
+        pltpu.make_async_copy(src, dst, sem_in.at[k])
+        for k, (src, dst) in enumerate(
+            [(wave_in, wave), (layer_in, layer), (agg_in, agg), (rhs_in, rhs), (cinv_in, cinv)]
+        )
+    ]
+    for load in loads:
+        load.start()
 
     def send(src, dst, kind, target):
         pltpu.make_async_remote_copy(
@@ -101,7 +121,10 @@
         magnitude = diag * diag + absorb * absorb
         return diag, absorb, damping * diag / magnitude, damping * absorb / magnitude
 
-    def own_rows(x, carry):
+    for load in loads[:4]:
+        load.wait()
+
+    def own_rows(x):
         for t in range(4):
             here = pl.ds(pl.multiple_of(row_of(x + HALO, t), 8), 8)
             there = pl.ds(8 * t, 8)
@@ -119,9 +142,8 @@
             si[here, :] = i
             z[0, 0, here, :] = rhs[0, x, there, :]
             z[0, 1, here, :] = rhs[1, x, there, :]
-        return carry
-
-    lax.fori_loop(0, NXD, own_rows, 0)
+
+    over_rows(0, NXD, 2, own_rows)
 
     def clear(k, carry):
         ag[pl.ds(pl.multiple_of(k * PITCH, 8), 8), :] = zero
@@ -155,12 +177,12 @@
                 high = pl.ds(row_of(HALO + NXD - width + s), NYD)
                 past = pl.ds(row_of(HALO + NXD + s), NYD)
                 ahead = pl.ds(row_of(HALO - width + s), NYD)
-                send(ref.at[low], ref.at[past], kind, beside_device(-1, 0))
-                send(ref.at[high], ref.at[ahead], kind, beside_device(1, 0))
+                send(ref.at[low], ref.at[past], kind, towards[-1, 0])
+                send(ref.at[high], ref.at[ahead], kind, towards[1, 0])
 
     def send_y(out, into, kind):
-        send(out.at[0], into.at[0], kind, beside_device(0, -1))
-        send(out.at[1], into.at[1], kind, beside_device(0, 1))
+        send(out.at[0], into.at[0], kind, towards[0, -1])
+        send(out.at[1], into.at[1], kind, towards[0, 1])
 
     def edge_row(dx, dy, ox, oy):
         x = ox if dx < 0 else NXD - 1 - ox
@@ -179,7 +201,7 @@
 
     def send_corners(out, into, kind):
         for k, (dx, dy) in enumerate(CORNERS):
-            send(out.at[k], into.at[3 - k], kind, beside_device(dx, dy))
+            send(out.at[k], into.at[3 - k], kind, towards[dx, dy])
 
     def unpack_corners(buf, cells):
         for k, (dx, dy) in enumerate(CORNERS):
@@ -191,7 +213,7 @@
     pack_y(iy_s, first_fields)
     pack_corners(ic_s, first_cells)
 
-    pl.semaphore_wait(barrier, len(DIRS) + 30)
+    pl.semaphore_wait(barrier, len(partners))
 
     send_x(first_fields, 0)
     send_y(iy_s, iy_r, 1)
@@ -213,6 +235,7 @@
             dim[at + 4] = jnp.where(low16, r_im, c_re)
         return carry
 
+    loads[4].wait()
     lax.fori_loop(0, 16, arrange, 0)
 
     take(u.at[0, 0, pl.ds(0, 22 * NYD)], sem_r.at[0])
@@ -285,28 +308,30 @@
         d, a = dg[here, :], ab[here, :]
         return c0, c1, d * c0 - b0 + a * c1, d * c1 - b1 - a * c0
 
-    def over_tiles(width, body):
+    def over_tiles(width, body, group):
         low = HALO - width
         body(row_of(low - 1, 4))
 
-        def rows(e, carry):
+        def row(e):
             for t in range(5):
                 body(pl.multiple_of(row_of(e, t), 8))
-            return carry
-
-        lax.fori_loop(low, HALO + NXD + width, rows, 0)
+
+        over_rows(low, HALO + NXD + width, group, row)
+
+    def put_first(here, a, b):
+        r, i = sr[here, :], si[here, :]
+        f[0, here, :] = r * a - i * b
+        f[1, here, :] = r * b + i * a
 
     def smooth_all(j):
         zj, mj, uj = z.at[j], m.at[j], u.at[j]
 
         def make_first(base):
             here = pl.ds(base, 8)
-            r, i = sr[here, :], si[here, :]
-            a, b = zj[0, here, :], zj[1, here, :]
-            f[0, here, :] = r * a - i * b
-            f[1, here, :] = r * b + i * a
-
-        over_tiles(2, make_first)
+            put_first(here, zj[0, here, :], zj[1, here, :])
+
+        if j == 0:
+            over_tiles(2, make_first, 4)
 
         def make_second(base):
             here = pl.ds(base, 8)
@@ -316,9 +341,9 @@
             mj[0, here, :] = f0 + (r * a - i * b)
             mj[1, here, :] = f1 + (r * b + i * a)
 
-        over_tiles(1, make_second)
-
-        def make_rest(x, carry):
+        over_tiles(1, make_second, 3)
+
+        def make_rest(x):
             for t in range(4):
                 base = pl.multiple_of(row_of(x + HALO, t), 8)
                 here = pl.ds(base, 8)
@@ -327,9 +352,8 @@
                 uj[1, here, :] = w1
                 rem[0, x, pl.ds(8 * t, 8), :] = zj[0, here, :] - w0
                 rem[1, x, pl.ds(8 * t, 8), :] = zj[1, here, :] - w1
-            return carry
-
-        lax.fori_loop(0, NXD, make_rest, 0)
+
+        over_rows(0, NXD, 4, make_rest)
 
     def restrict():
         def rows(x, sums):
@@ -365,7 +389,7 @@
                     sums[2 + 2 * i] = sums[2 + 2 * i] + (c * b - d * a)
             return tuple(sums)
 
-        sums = lax.fori_loop(0, NXD, rows, (zero,) * (1 + 2 * j))
+        sums = lax.fori_loop(0, NXD // 2, lambda k, c: rows(2 * k + 1, rows(2 * k, c)), (zero,) * (1 + 2 * j))
         out = zero
         for k, total in enumerate(sums):
             out = out + jnp.where(lane == k, jnp.sum(total, axis=1, keepdims=True), 0.0)
@@ -378,11 +402,8 @@
         g1[j, 2 * s1] = coarse if coarse is not None else jnp.zeros((1, 128), F32)
         g1[j, 2 * s1 + 1] = dots
 
-        def step(k, carry):
-            send(mine, mine, S1 + j, member1(k))
-            return carry
-
-        lax.fori_loop(1, 16, step, 0)
+        for target in group1:
+            send(mine, mine, S1 + j, target)
 
     def middle_gather(j):
         take(g1.at[j, pl.ds(0, 30)], sem_r.at[S1 + j])
@@ -396,11 +417,8 @@
         g2[j, 5 * s2 + 4] = total
         mine = g2.at[j, pl.ds(5 * s2, 5)]
 
-        def step(k, carry):
-            send(mine, mine, S2 + j, member2(k))
-            return carry
-
-        lax.fori_loop(1, 16, step, 0)
+        for target in group2:
+            send(mine, mine, S2 + j, target)
 
     def end_gather(j):
         take(g2.at[j, pl.ds(0, 75)], sem_r.at[S2 + j])
@@ -418,15 +436,17 @@
 
     def coarse_solve(j):
         def step(k, sums):
-            a, b = sums
-            for q in range(4):
-                row = g2[j, 5 * k + q]
-                a = a + dre[4 * k + q] * row
-                b = b + dim[4 * k + q] * row
-            return a, b
-
-        empty = jnp.zeros((16, 128), F32)
-        a, b = lax.fori_loop(0, 16, step, (empty, empty))
+            sums = list(sums)
+            for o in range(4):
+                for q in range(4):
+                    row = g2[j, 20 * k + 5 * o + q]
+                    at = 16 * k + 4 * o + q
+                    sums[q % 2] = sums[q % 2] + dre[at] * row
+                    sums[2 + q % 2] = sums[2 + q % 2] + dim[at] * row
+            return tuple(sums)
+
+        sums = lax.fori_loop(0, 4, step, (jnp.zeros((16, 128), F32),) * 4)
+        a, b = sums[0] + sums[1], sums[2] + sums[3]
         own = lane16 == sub16
         re = jnp.sum(
             jnp.where(own, jnp.sum(a, axis=1, keepdims=True), 0.0), axis=0, keepdims=True
@@ -436,7 +456,7 @@
         )
         cown[j, 0] = re + pltpu.roll(jnp.broadcast_to(im, (8, 128)), 16, axis=1)[0:1]
         for k, (dx, dy) in enumerate(DIRS):
-            send(cown.at[j], crecv.at[j, pl.ds(7 - k, 1)], CX + j, beside_device(dx, dy))
+            send(cown.at[j], crecv.at[j, pl.ds(7 - k, 1)], CX + j, towards[dx, dy])
         return re, im
 
     def spread(table, here):
@@ -446,7 +466,37 @@
             jnp.take_along_axis(table, which + 16, axis=1, mode="promise_in_bounds"),
         )
 
-    def prolong(j):
+    def place(table, base):
+        here = pl.ds(base, 8)
+        a, b = spread(table, here)
+        p[0, here, :] = a
+        p[1, here, :] = b
+
+    def clear_halo():
+        def clear_tile(base):
+            here = pl.ds(base, 8)
+            p[0, here, :] = zero
+            p[1, here, :] = zero
+
+        over_halo(3, clear_tile)
+
+    def over_halo(width, body):
+        low = HALO - width
+        body(row_of(low - 1, 4))
+        for e in [*range(low, HALO), *range(HALO + NXD, HALO + NXD + width)]:
+            for t in range(5):
+                body(row_of(e, t))
+
+        def edge(e):
+            body(pl.multiple_of(row_of(e, 4), 8))
+
+        over_rows(HALO, HALO + NXD, 8, edge)
+
+    def prolong_own(j):
+        table = jnp.broadcast_to(cown[j, 0], (8, 128))
+        over_own(functools.partial(place, table))
+
+    def prolong_halo(j):
         take(crecv.at[j], sem_r.at[CX + j])
 
         def row(dx, dy):
@@ -454,12 +504,6 @@
                 return jnp.broadcast_to(cown[j, 0], (8, 128))
             return jnp.broadcast_to(crecv[j, DIRS.index((dx, dy))], (8, 128))
 
-        def place(table, base):
-            here = pl.ds(base, 8)
-            a, b = spread(table, here)
-            p[0, here, :] = a
-            p[1, here, :] = b
-
         def side(e):
             return -1 if e < HALO else (1 if e >= HALO + NXD else 0)
 
@@ -467,20 +511,18 @@
             return jnp.where(sub < 4, row(side(e), 1), row(side(e + 1), -1))
 
         place(halo_table(-1), row_of(-1, 4))
-        for e in [0, 1, 2, 18, 19, 20, 21]:
+        for e in [0, 1, 2, 19, 20, 21]:
             table = row(side(e), 0)
             for t in range(4):
                 place(table, row_of(e, t))
             place(halo_table(e), row_of(e, 4))
-        table, edge = row(0, 0), halo_table(HALO)
-
-        def rows(e, carry):
-            for t in range(4):
-                place(table, pl.multiple_of(row_of(e, t), 8))
+        place(halo_table(18), row_of(18, 4))
+        edge = halo_table(HALO)
+
+        def middle(e):
             place(edge, pl.multiple_of(row_of(e, 4), 8))
-            return carry
-
-        lax.fori_loop(3, 18, rows, 0)
+
+        over_rows(3, 18, 5, middle)
 
     def send_halo(j):
         fields = [(u.at[j, 0], 2), (u.at[j, 1], 2)]
@@ -501,12 +543,11 @@
         unpack_corners(uc_r.at[j], cells)
 
     def over_own(body):
-        def rows(x, carry):
+        def row(x):
             for t in range(4):
                 body(pl.multiple_of(row_of(x + HALO, t), 8))
-            return carry
-
-        lax.fori_loop(0, NXD, rows, 0)
+
+        over_rows(0, NXD, 4, row)
 
     columns = []
     lengths = []
@@ -528,6 +569,7 @@
         if j + 1 < ITERS:
             send_halo(j)
         middle_gather(j)
+        clear_halo()
         if j + 1 < ITERS:
             take_halo(j)
         dots = end_gather(j)
@@ -546,8 +588,6 @@
             v[j, 0, here, :] = a * inverse
             v[j, 1, here, :] = b * inverse
 
-        over_own(make_basis)
-
         def make_start(base):
             here = pl.ds(base, 8)
             a, b = u[j, 0, here, :], u[j, 1, here, :]
@@ -559,21 +599,57 @@
             z[j + 1, 1, here, :] = b
 
         if j + 1 < ITERS:
-            over_tiles(2, make_start)
+            over_tiles(2, make_start, 4)
         else:
             over_own(make_start)
-        prolong(j)
+        zn = z.at[j + 1]
+        last = j + 1 == ITERS
 
         def make_image(base):
             here = pl.ds(base, 8)
             _, _, w0, w1 = operate(p, base)
-            z[j + 1, 0, here, :] = (z[j + 1, 0, here, :] + w0) * inverse
-            z[j + 1, 1, here, :] = (z[j + 1, 1, here, :] + w1) * inverse
-
-        if j + 1 < ITERS:
-            over_tiles(2, make_image)
-        else:
-            over_own(make_image)
+            a, b = (zn[0, here, :] + w0) * inverse, (zn[1, here, :] + w1) * inverse
+            zn[0, here, :] = a
+            zn[1, here, :] = b
+            if not last:
+                put_first(here, a, b)
+
+        prolong_own(j)
+        over_own(make_image)
+        over_own(make_basis)
+        prolong_halo(j)
+        if not last:
+            over_halo(2, make_image)
+
+        def add_edges(e, t, shifts):
+            base = row_of(e, t)
+            if not isinstance(e, int):
+                base = pl.multiple_of(base, 8)
+            here = pl.ds(base, 8)
+            parts = [zn[0, here, :], zn[1, here, :]]
+            for c in range(2):
+                for shift in shifts:
+                    beyond = p[c, pl.ds(base + shift, 8), :]
+                    if shift == 1:
+                        beyond = jnp.where(sub == 7, beyond, 0.0)
+                    if shift == -1:
+                        beyond = jnp.where(sub == 0, beyond, 0.0)
+                    parts[c] = parts[c] - beyond * inverse
+                zn[c, here, :] = parts[c]
+            if not last:
+                put_first(here, parts[0], parts[1])
+
+        for e, shift in ((HALO, -PITCH), (HALO + NXD - 1, PITCH)):
+            add_edges(e, 0, (shift, -1))
+            add_edges(e, 1, (shift,))
+            add_edges(e, 2, (shift,))
+            add_edges(e, 3, (shift, 1))
+
+        def y_edges(e):
+            add_edges(e, 0, (-1,))
+            add_edges(e, 3, (1,))
+
+        over_rows(HALO + 1, HALO + NXD - 1, 7, y_edges)
 
     start_gather(ITERS, None, products(ITERS))
     middle_gather(ITERS)
@@ -629,7 +705,7 @@
         c_im = c_im + (wr * coarse[j][1] + wi * coarse[j][0])
     table = c_re + pltpu.roll(c_im, 16, axis=1)
 
-    def write(x, carry):
+    def write(x):
         for t in range(4):
             here = pl.ds(pl.multiple_of(row_of(x + HALO, t), 8), 8)
             a, b = spread(table, here)
@@ -640,19 +716,18 @@
                 b = b + (wr * d + wi * c)
             sol[0, x, pl.ds(8 * t, 8), :] = a
             sol[1, x, pl.ds(8 * t, 8), :] = b
-        return carry
-
-    lax.fori_loop(0, NXD, write, 0)
+
+    over_rows(0, NXD, 4, write)
 
     h_re, h_im = zero, zero
     for j in range(ITERS):
         for i, (re, im) in enumerate(columns[j]):
-            spot = (sub == i) & (lane == j)
+            spot = (sub == j) & (lane == i)
             h_re = jnp.where(spot, re, h_re)
             h_im = jnp.where(spot, im, h_im)
-        h_re = jnp.where((sub == j + 1) & (lane == j), lengths[j + 1], h_re)
-    hess[0] = h_re
-    hess[1] = h_im
+        h_re = jnp.where((sub == j) & (lane == j + 1), lengths[j + 1], h_re)
+    hess[0] = h_re[:ITERS, : ITERS + 1]
+    hess[1] = h_im[:ITERS, : ITERS + 1]
 
     take(u.at[0, 0, pl.ds(0, 22 * NYD)], sem_s.at[0])
     take(iy_s, sem_s.at[1])
@@ -668,7 +743,7 @@
             take(uc_s.at[j], sem_s.at[UC + j])
 
 
-def body(right_side, wavenumber, pml_layer, aggregate, coarse_inverse):
+def body(*args):
     field = pltpu.VMEM((2, ROWS, 128), F32)
     plane = pltpu.VMEM((ROWS, 128), F32)
 
@@ -679,12 +754,13 @@
     solution, hessenberg = pl.pallas_call(
         kernel,
         out_shape=(
-            jax.ShapeDtypeStruct(right_side.shape, F32),
-            jax.ShapeDtypeStruct((2, 8, 128), F32),
+            jax.ShapeDtypeStruct(args[0].shape, F32),
+            jax.ShapeDtypeStruct((2, ITERS, ITERS + 1), F32),
         ),
-        in_specs=[vmem] * 5,
+        in_specs=[pl.BlockSpec(memory_space=pl.ANY)] * 5,
         out_specs=(vmem, vmem),
         scratch_shapes=[
+            *[pltpu.VMEM(a.shape, a.dtype) for a in args],
             *[plane] * 7,
             pltpu.VMEM((ROWS, 128), jnp.int32),
             fields(5), fields(4), fields(4), fields(4),
@@ -706,12 +782,13 @@
             pltpu.VMEM((3, 4, 8, 128), F32),
             pltpu.SemaphoreType.DMA((28,)),
             pltpu.SemaphoreType.DMA((28,)),
+            pltpu.SemaphoreType.DMA((5,)),
         ],
         compiler_params=pltpu.CompilerParams(
             collective_id=0, has_side_effects=True, vmem_limit_bytes=60 * 1024 * 1024
         ),
-    )(right_side, wavenumber, pml_layer, aggregate, coarse_inverse)
-    return solution, hessenberg[:, : ITERS + 1, :ITERS]
+    )(*args)
+    return solution, hessenberg.transpose(0, 2, 1)
 
 
 def solution(mesh):

time: 132 us -> 109 us (0.83)
  Pallas kernels: 128 us -> 106 us
    pallas_call x1, Pallas kernels: 128 us -> 106 us  [body(): pl.pallas_call(kernel, out_shape=(jax.ShapeDtypeStruct(args[0].shape, F32...]
    unnamed x2 -> x4, local copies, waits for them, and re-layouts: 3.24 us -> 2.47 us
where the time goes in v2:
time: 109 us
  Pallas kernels  106 us (97%)
  local copies, waits for them, and re-layouts  2.47 us (2%)
    pallas_call x1, Pallas kernels, body(): pl.pallas_call(kernel, out_shape=(jax.ShapeDtypeStruct(args[0].shape, F32...  106 us
    unnamed x4, local copies, waits for them, and re-layouts  2.47 us

profile of v2, /device:TPU:1, one launch (start us, length us, event | category | flops | bytes accessed | tf_op | source)
XLA Modules:
  0.0 109.1 jit_solution(7901150629382041139)
XLA Ops:
  0.6 106.0 %shard_map.68 = (f32[2,16,32,128]{3,2,1,0:T(8,128)}, f32[2,4,5]{2,1,0:T(4,128)}) custom-call(f32[2,16,32,128]{3,2,1,0:T(8,128)} %rhs_in.1, f32[16,32,128]{2,1,0:T(8,128)} %wave_in.1, s32[16,32,128]{2,1,0:T(8,128)} %layer_in.1, s32[16,32,128]{2,1,0:T(8,128)} %agg_in.1, f32[2,16,4096]{2,1,0:T(8,128)} %cinv_in.1), custom_call_target="tpu_custom_call" | custom-call | tf_op jit(solution)/shard_map/pallas_call | solution.py:754
  106.6 0.0 copy-start
  106.6 1.9 %copy.9 = f32[2,16,32,128]{3,2,1,0:T(8,128)} copy(f32[2,16,32,128]{3,2,1,0:T(8,128)} %get-tuple-element.8) | data formatting | bytes 1048576
  108.5 0.0 copy-done
  108.5 0.6 copy.10
Async XLA Ops:
  106.6 1.9 %copy-start = (f32[2,4,5]{2,1,0:T(4,128)S(1)}, f32[2,4,5]{2,1,0:T(4,128)}, u32[]{:S(2)}) copy-start(f32[2,4,5]{2,1,0:T(4,128)} %get-tuple-element.5) | copy-start | bytes 484

commit v3 on v2

--- a/solution.py
+++ b/solution.py
@@ -46,9 +46,9 @@
     sol, hess,
     rhs, wave, layer, agg, cinv,
     wv, lf, ag, dg, ab, sr, si, idx,
-    z, u, m, v, f, p, rem,
+    z, u, m, v, f, p, rem, parts,
     dre, dim, g1, g2, cown, crecv,
-    iy_s, iy_r, ic_s, ic_r, uy_s, uy_r, uc_s, uc_r,
+    iy_s, iy_r, ic_s, ic_r, ly_s, ly_r, lc_s, lc_r, uy_s, uy_r, uc_s, uc_r,
     sem_s, sem_r, sem_in,
 ):
     zh, px, co = lax.axis_index("zh"), lax.axis_index("px"), lax.axis_index("co")
@@ -140,8 +140,11 @@
             ab[here, :] = a
             sr[here, :] = r
             si[here, :] = i
-            z[0, 0, here, :] = rhs[0, x, there, :]
-            z[0, 1, here, :] = rhs[1, x, there, :]
+            z0, z1 = rhs[0, x, there, :], rhs[1, x, there, :]
+            z[0, 0, here, :] = z0
+            z[0, 1, here, :] = z1
+            f[0, here, :] = r * z0 - i * z1
+            f[1, here, :] = r * z1 + i * z0
 
     over_rows(0, NXD, 2, own_rows)
 
@@ -151,34 +154,57 @@
 
     lax.fori_loop(0, NXD + 2 * HALO + 1, clear, 0)
 
+    def no_rows(first):
+        for ref in (wv, lf, ag, *[r.at[c] for r in (f, z.at[0], u.at[0], u.at[1], u.at[2]) for c in (0, 1)]):
+            for e in range(first, first + HALO):
+                for t in range(4):
+                    ref[pl.ds(row_of(e, t), 8), :] = zero
+
+    pl.when(gx == 0)(lambda: no_rows(0))
+    pl.when(gx == 15)(lambda: no_rows(HALO + NXD))
+
     def y_columns(ref, y):
         return ref[pl.ds(row_of(HALO) + y, NXD, stride=PITCH), :]
 
     def pack_y(buf, fields):
-        at = 0
-        for ref, width in fields:
-            for s in range(width):
-                buf[0, at] = y_columns(ref, s)
-                buf[1, at] = y_columns(ref, NYD - width + s)
-                at += 1
-
-    def unpack_y(buf, fields):
-        at = 0
-        for ref, width in fields:
-            for s in range(width):
-                ref[pl.ds(row_of(HALO) + NYD + s, NXD, stride=PITCH), :] = buf[0, at]
-                ref[pl.ds(row_of(HALO) - width + s, NXD, stride=PITCH), :] = buf[1, at]
-                at += 1
+        for at, (ref, d) in enumerate(fields):
+            buf[0, at] = y_columns(ref, d)
+            buf[1, at] = y_columns(ref, NYD - 1 - d)
+
+    def unpack_y(buf, fields, which):
+        for at, (ref, d) in enumerate(fields):
+            if which(at):
+                ref[pl.ds(row_of(HALO) + NYD + d, NXD, stride=PITCH), :] = buf[0, at]
+                ref[pl.ds(row_of(HALO) - 1 - d, NXD, stride=PITCH), :] = buf[1, at]
 
     def send_x(fields, kind):
-        for ref, width in fields:
-            for s in range(width):
-                low = pl.ds(row_of(HALO + s), NYD)
-                high = pl.ds(row_of(HALO + NXD - width + s), NYD)
-                past = pl.ds(row_of(HALO + NXD + s), NYD)
-                ahead = pl.ds(row_of(HALO - width + s), NYD)
-                send(ref.at[low], ref.at[past], kind, towards[-1, 0])
-                send(ref.at[high], ref.at[ahead], kind, towards[1, 0])
+        def rows(e):
+            return pl.ds(row_of(e), NYD)
+
+        @pl.when(gx > 0)
+        def _():
+            for ref, d in fields:
+                send(
+                    ref.at[rows(HALO + d)], ref.at[rows(HALO + NXD + d)], kind + 1, towards[-1, 0]
+                )
+
+        @pl.when(gx < 15)
+        def _():
+            for ref, d in fields:
+                send(
+                    ref.at[rows(HALO + NXD - 1 - d)], ref.at[rows(HALO - 1 - d)], kind,
+                    towards[1, 0],
+                )
+
+    def take_x(fields, kind):
+        like = u.at[0, 0, pl.ds(0, len(fields) * NYD)]
+        pl.when(gx > 0)(lambda: take(like, sem_r.at[kind]))
+        pl.when(gx < 15)(lambda: take(like, sem_r.at[kind + 1]))
+
+    def take_sent_x(fields, kind):
+        like = u.at[0, 0, pl.ds(0, len(fields) * NYD)]
+        pl.when(gx > 0)(lambda: take(like, sem_s.at[kind + 1]))
+        pl.when(gx < 15)(lambda: take(like, sem_s.at[kind]))
 
     def send_y(out, into, kind):
         send(out.at[0], into.at[0], kind, towards[0, -1])
@@ -208,16 +234,24 @@
             for at, (ref, ox, oy) in enumerate(cells):
                 ref[pl.ds(past_row(dx, dy, ox, oy), 1), :] = buf[k, pl.ds(at, 1), :]
 
-    first_fields = [(z.at[0, 0], 2), (z.at[0, 1], 2), (wv, 2), (lf, 2), (ag, 3)]
-    first_cells = [(ref, 0, 0) for ref, _ in first_fields] + [(ag, 1, 0), (ag, 0, 1)]
-    pack_y(iy_s, first_fields)
-    pack_corners(ic_s, first_cells)
+    E0, E1, EU = 14, 18, 22
+    soon = [(z.at[0, 0], 0), (z.at[0, 1], 0), (wv, 0), (lf, 0), (f.at[0], 1), (f.at[1], 1)]
+    soon_cells = [(f.at[0], 0, 0), (f.at[1], 0, 0)]
+    late = [(wv, 1), (lf, 1), (ag, 0), (ag, 1), (ag, 2)]
+    late_cells = [(wv, 0, 0), (lf, 0, 0), (ag, 0, 0), (ag, 1, 0), (ag, 0, 1)]
+    pack_y(iy_s, soon)
+    pack_corners(ic_s, soon_cells)
+    pack_y(ly_s, late)
+    pack_corners(lc_s, late_cells)
 
     pl.semaphore_wait(barrier, len(partners))
 
-    send_x(first_fields, 0)
-    send_y(iy_s, iy_r, 1)
-    send_corners(ic_s, ic_r, 2)
+    send_x(soon, E0)
+    send_y(iy_s, iy_r, E0 + 2)
+    send_corners(ic_s, ic_r, E0 + 3)
+    send_x(late, E1)
+    send_y(ly_s, ly_r, E1 + 2)
+    send_corners(lc_s, lc_r, E1 + 3)
 
     lane16 = lax.broadcasted_iota(jnp.int32, (16, 128), 1)
     low16 = lane16 < 64
@@ -238,12 +272,6 @@
     loads[4].wait()
     lax.fori_loop(0, 16, arrange, 0)
 
-    take(u.at[0, 0, pl.ds(0, 22 * NYD)], sem_r.at[0])
-    take(iy_r, sem_r.at[1])
-    take(ic_r, sem_r.at[2])
-    unpack_y(iy_r, first_fields)
-    unpack_corners(ic_r, first_cells)
-
     def x_inside(e):
         below = jnp.where(gx > 0, 1, 0)
         above = jnp.where(gx < 15, 1, 0)
@@ -252,13 +280,15 @@
     y_up = jnp.where(gy < 15, 1, 0)
     y_down = jnp.where(gy > 0, 1, 0)
 
-    def halo_tile(e, t, with_coefficients):
-        here = pl.ds(pl.multiple_of(row_of(e, t), 8), 8)
+    def halo_tile(e, t, with_index, with_coefficients):
+        base = row_of(e, t)
+        here = pl.ds(base if isinstance(e, int) else pl.multiple_of(base, 8), 8)
         if t < 4:
             inside = jnp.full((8, 128), x_inside(e), jnp.int32) > 0
         else:
             inside = jnp.where(sub < 4, x_inside(e) * y_up, x_inside(e + 1) * y_down) > 0
-        idx[here, :] = jnp.where(inside, ag[here, :].astype(jnp.int32), 32)
+        if with_index:
+            idx[here, :] = jnp.where(inside, ag[here, :].astype(jnp.int32), 32)
         if with_coefficients:
             d, a, r, i = coefficients(wv[here, :], lf[here, :])
             dg[here, :] = d
@@ -266,28 +296,57 @@
             sr[here, :] = jnp.where(inside, r, 0.0)
             si[here, :] = jnp.where(inside, i, 0.0)
 
-    def y_halos(e, carry):
-        halo_tile(e, 4, True)
-        return carry
-
-    halo_tile(-1, 4, False)
-    lax.fori_loop(0, 21, y_halos, 0)
-    halo_tile(21, 4, False)
-    for low_e in (0, 19):
-
-        def x_halos(k, carry):
-            for t in range(4):
-                halo_tile(low_e + k, t, True)
-            return carry
-
-        if low_e == 0:
-            for t in range(4):
-                halo_tile(0, t, False)
-            lax.fori_loop(1, 3, x_halos, 0)
-        else:
-            lax.fori_loop(0, 2, x_halos, 0)
-            for t in range(4):
-                halo_tile(21, t, False)
+    def each_halo(width, body):
+        low = HALO - width
+        body(low - 1, 4)
+        for e in [*range(low, HALO), *range(HALO + NXD, HALO + NXD + width)]:
+            for t in range(5):
+                body(e, t)
+
+        def edge(e):
+            body(e, 4)
+
+        over_rows(HALO, HALO + NXD, 8, edge)
+
+    def over_halo(width, body):
+        def tile(e, t):
+            base = row_of(e, t)
+            body(base if isinstance(e, int) else pl.multiple_of(base, 8))
+
+        each_halo(width, tile)
+
+    def put_first(here, a, b):
+        r, i = sr[here, :], si[here, :]
+        f[0, here, :] = r * a - i * b
+        f[1, here, :] = r * b + i * a
+
+    take_x(soon, E0)
+    take(iy_r, sem_r.at[E0 + 2])
+    take(ic_r, sem_r.at[E0 + 3])
+    unpack_y(iy_r, soon, lambda at: at < 4)
+    each_halo(1, lambda e, t: halo_tile(e, t, False, True))
+
+    def halo_first(base):
+        here = pl.ds(base, 8)
+        put_first(here, z[0, 0, here, :], z[0, 1, here, :])
+
+    over_halo(1, halo_first)
+    unpack_y(iy_r, soon, lambda at: at >= 4)
+    for k, (dx, dy) in enumerate(CORNERS):
+        there = x_inside(-1 if dx < 0 else HALO + NXD) * (y_down if dy < 0 else y_up)
+        there = jnp.full((8, 128), there, jnp.int32) > 0
+        ic_r[k] = jnp.where(there, ic_r[k], 0.0)
+    unpack_corners(ic_r, soon_cells)
+
+    def take_late():
+        take_sent_x(soon, E0)
+        take_x(late, E1)
+        take(ly_r, sem_r.at[E1 + 2])
+        take(lc_r, sem_r.at[E1 + 3])
+        unpack_y(ly_r, late, lambda at: True)
+        unpack_corners(lc_r, late_cells)
+        each_halo(2, lambda e, t: halo_tile(e, t, False, True))
+        each_halo(3, lambda e, t: halo_tile(e, t, True, False))
 
     def neighbours(ref, c, base):
         centre = ref[c, pl.ds(base, 8), :]
@@ -318,84 +377,124 @@
 
         over_rows(low, HALO + NXD + width, group, row)
 
-    def put_first(here, a, b):
-        r, i = sr[here, :], si[here, :]
-        f[0, here, :] = r * a - i * b
-        f[1, here, :] = r * b + i * a
-
-    def smooth_all(j):
-        zj, mj, uj = z.at[j], m.at[j], u.at[j]
-
-        def make_first(base):
+    four, five = (0, 1, 2, 3), (0, 1, 2, 3, 4)
+    ALL = [(3, 19, 4, four)]
+    INNER_SECOND = [(5, 17, 4, four)]
+    OUTER_SECOND = [(2, 5, 3, five), (17, 20, 3, five), (5, 17, 4, (0, 3, 4))]
+    INNER_REST = [(6, 16, 5, (1, 2))]
+    OUTER_REST = [(3, 6, 3, four), (16, 19, 3, four), (6, 16, 5, (0, 3))]
+    INNER_DOTS = [(4, 18, 7, (1, 2))]
+    OUTER_DOTS = [(3, 4, 1, four), (18, 19, 1, four), (4, 18, 7, (0, 3))]
+
+    def sweep(tiles, body):
+        for low, high, group, ts in tiles:
+
+            def row(e, ts=ts):
+                for t in ts:
+                    body(pl.multiple_of(row_of(e, t), 8), e, t)
+
+            over_rows(low, high, group, row)
+
+    def sweep_sums(tiles, sums, add):
+        for low, high, group, ts in tiles:
+
+            def trip(k, carry, low=low, group=group, ts=ts):
+                carry = list(carry)
+                for q in range(group):
+                    for t in ts:
+                        e = low + k * group + q
+                        add(carry, pl.multiple_of(row_of(e, t), 8), e, t)
+                return tuple(carry)
+
+            sums = lax.fori_loop(0, (high - low) // group, trip, tuple(sums))
+        return sums
+
+    def there(e, t):
+        return pl.ds(pl.multiple_of((e - HALO) * NYD + 8 * t, 8), 8)
+
+    def make_second(j):
+        def body(base, e=None, t=None):
             here = pl.ds(base, 8)
-            put_first(here, zj[0, here, :], zj[1, here, :])
-
-        if j == 0:
-            over_tiles(2, make_first, 4)
-
-        def make_second(base):
+            f0, b0 = neighbours(f, 0, base)
+            f1, b1 = neighbours(f, 1, base)
+            r, i = sr[here, :], si[here, :]
+            m[j, 0, here, :] = (2.0 - damping) * f0 + (r * b0 - i * b1)
+            m[j, 1, here, :] = (2.0 - damping) * f1 + (r * b1 + i * b0)
+
+        return body
+
+    def make_rest(j):
+        def body(base, e, t):
             here = pl.ds(base, 8)
-            f0, f1, w0, w1 = operate(f, base)
-            r, i = sr[here, :], si[here, :]
-            a, b = zj[0, here, :] - w0, zj[1, here, :] - w1
-            mj[0, here, :] = f0 + (r * a - i * b)
-            mj[1, here, :] = f1 + (r * b + i * a)
-
-        over_tiles(1, make_second, 3)
-
-        def make_rest(x):
-            for t in range(4):
-                base = pl.multiple_of(row_of(x + HALO, t), 8)
-                here = pl.ds(base, 8)
-                _, _, w0, w1 = operate(mj, base)
-                uj[0, here, :] = w0
-                uj[1, here, :] = w1
-                rem[0, x, pl.ds(8 * t, 8), :] = zj[0, here, :] - w0
-                rem[1, x, pl.ds(8 * t, 8), :] = zj[1, here, :] - w1
-
-        over_rows(0, NXD, 4, make_rest)
-
-    def restrict():
-        def rows(x, sums):
-            sums = list(sums)
-            for t in range(4):
-                which = idx[pl.ds(pl.multiple_of(row_of(x + HALO, t), 8), 8), :]
-                a, b = rem[0, x, pl.ds(8 * t, 8), :], rem[1, x, pl.ds(8 * t, 8), :]
-                for g in range(16):
-                    mask = which == g
-                    sums[g] = sums[g] + jnp.where(mask, a, 0.0)
-                    sums[16 + g] = sums[16 + g] + jnp.where(mask, b, 0.0)
-            return tuple(sums)
-
-        sums = lax.fori_loop(0, NXD, rows, (zero,) * 32)
+            _, _, w0, w1 = operate(m.at[j], base)
+            u[j, 0, here, :] = w0
+            u[j, 1, here, :] = w1
+            rem[0, there(e, t), :] = z[j, 0, here, :] - w0
+            rem[1, there(e, t), :] = z[j, 1, here, :] - w1
+
+        return body
+
+    def add_restricted(sums, base, e, t):
+        which = idx[pl.ds(base, 8), :]
+        a, b = rem[0, there(e, t), :], rem[1, there(e, t), :]
+        for g in range(16):
+            mask = which == g
+            sums[g] = sums[g] + jnp.where(mask, a, 0.0)
+            sums[16 + g] = sums[16 + g] + jnp.where(mask, b, 0.0)
+
+    def add_products(j):
+        def add(sums, base, e, t):
+            here = pl.ds(base, 8)
+            a, b = z[j, 0, here, :], z[j, 1, here, :]
+            sums[0] = sums[0] + (a * a + b * b)
+            for i in range(j):
+                c, d = v[i, 0, here, :], v[i, 1, here, :]
+                sums[1 + 2 * i] = sums[1 + 2 * i] + (c * a + d * b)
+                sums[2 + 2 * i] = sums[2 + 2 * i] + (c * b - d * a)
+
+        return add
+
+    def in_lanes(sums, lane_of):
         out = zero
-        for k in range(32):
-            place = (k // 16) * 64 + k % 16
+        for k, total in enumerate(sums):
             out = out + jnp.where(
-                lane == zl * 16 + place, jnp.sum(sums[k], axis=1, keepdims=True), 0.0
+                lane == lane_of(k), jnp.sum(total, axis=1, keepdims=True), 0.0
             )
         return jnp.sum(out, axis=0, keepdims=True)
 
-    def products(j):
-        def rows(x, sums):
-            sums = list(sums)
-            for t in range(4):
-                here = pl.ds(pl.multiple_of(row_of(x + HALO, t), 8), 8)
-                a, b = z[j, 0, here, :], z[j, 1, here, :]
-                sums[0] = sums[0] + (a * a + b * b)
-                for i in range(j):
-                    c, d = v[i, 0, here, :], v[i, 1, here, :]
-                    sums[1 + 2 * i] = sums[1 + 2 * i] + (c * a + d * b)
-                    sums[2 + 2 * i] = sums[2 + 2 * i] + (c * b - d * a)
-            return tuple(sums)
-
-        sums = lax.fori_loop(0, NXD // 2, lambda k, c: rows(2 * k + 1, rows(2 * k, c)), (zero,) * (1 + 2 * j))
-        out = zero
+    def keep(sums, at):
         for k, total in enumerate(sums):
-            out = out + jnp.where(lane == k, jnp.sum(total, axis=1, keepdims=True), 0.0)
-        return jnp.sum(out, axis=0, keepdims=True)
-
-    S1, S2, CX, UX, UY, UC = 3, 8, 13, 17, 21, 25
+            parts[at + k] = total
+
+    def kept(count, at):
+        return [parts[at + k] for k in range(count)]
+
+    def inner(j):
+        if j < ITERS:
+            sweep(INNER_SECOND, make_second(j))
+            sweep(INNER_REST, make_rest(j))
+            keep(sweep_sums(INNER_REST, [zero] * 32, add_restricted), 0)
+        keep(sweep_sums(INNER_DOTS, [zero] * (1 + 2 * j), add_products(j)), 32)
+
+    def outer(j):
+        restricted = None
+        if j == 0:
+            over_tiles(1, make_second(0), 3)
+            sweep(ALL, make_rest(0))
+            restricted = sweep_sums(ALL, [zero] * 32, add_restricted)
+            dots = sweep_sums(ALL, [zero], add_products(0))
+        else:
+            if j < ITERS:
+                make_second(j)(row_of(1, 4))
+                sweep(OUTER_SECOND, make_second(j))
+                sweep(OUTER_REST, make_rest(j))
+                restricted = sweep_sums(OUTER_REST, kept(32, 0), add_restricted)
+            dots = sweep_sums(OUTER_DOTS, kept(1 + 2 * j, 32), add_products(j))
+        if restricted is not None:
+            restricted = in_lanes(restricted, lambda k: zl * 16 + (k // 16) * 64 + k % 16)
+        start_gather(j, restricted, in_lanes(dots, lambda k: k))
+
+    S1, S2, CX = 0, 5, 10
 
     def start_gather(j, coarse, dots):
         mine = g1.at[j, pl.ds(2 * s1, 2)]
@@ -422,6 +521,8 @@
 
     def end_gather(j):
         take(g2.at[j, pl.ds(0, 75)], sem_r.at[S2 + j])
+
+    def all_products(j):
         total = g2[j, 4]
         for s in range(1, 16):
             total = total + g2[j, 5 * s + 4]
@@ -447,17 +548,12 @@
 
         sums = lax.fori_loop(0, 4, step, (jnp.zeros((16, 128), F32),) * 4)
         a, b = sums[0] + sums[1], sums[2] + sums[3]
-        own = lane16 == sub16
-        re = jnp.sum(
-            jnp.where(own, jnp.sum(a, axis=1, keepdims=True), 0.0), axis=0, keepdims=True
-        )
-        im = jnp.sum(
-            jnp.where(own, jnp.sum(b, axis=1, keepdims=True), 0.0), axis=0, keepdims=True
-        )
-        cown[j, 0] = re + pltpu.roll(jnp.broadcast_to(im, (8, 128)), 16, axis=1)[0:1]
+        a = jnp.sum(a, axis=1, keepdims=True)
+        b = jnp.sum(b, axis=1, keepdims=True)
+        both = jnp.where(lane16 == sub16, a, 0.0) + jnp.where(lane16 == sub16 + 16, b, 0.0)
+        cown[j, 0] = jnp.sum(both, axis=0, keepdims=True)
         for k, (dx, dy) in enumerate(DIRS):
             send(cown.at[j], crecv.at[j, pl.ds(7 - k, 1)], CX + j, towards[dx, dy])
-        return re, im
 
     def spread(table, here):
         which = idx[here, :]
@@ -479,18 +575,6 @@
             p[1, here, :] = zero
 
         over_halo(3, clear_tile)
-
-    def over_halo(width, body):
-        low = HALO - width
-        body(row_of(low - 1, 4))
-        for e in [*range(low, HALO), *range(HALO + NXD, HALO + NXD + width)]:
-            for t in range(5):
-                body(row_of(e, t))
-
-        def edge(e):
-            body(pl.multiple_of(row_of(e, 4), 8))
-
-        over_rows(HALO, HALO + NXD, 8, edge)
 
     def prolong_own(j):
         table = jnp.broadcast_to(cown[j, 0], (8, 128))
@@ -524,22 +608,26 @@
 
         over_rows(3, 18, 5, middle)
 
+    def image_fields(j):
+        return (
+            [(u.at[j, c], d) for d in (0, 1) for c in (0, 1)],
+            [(u.at[j, 0], 0, 0), (u.at[j, 1], 0, 0)],
+        )
+
     def send_halo(j):
-        fields = [(u.at[j, 0], 2), (u.at[j, 1], 2)]
-        cells = [(u.at[j, 0], 0, 0), (u.at[j, 1], 0, 0)]
+        fields, cells = image_fields(j)
         pack_y(uy_s.at[j], fields)
         pack_corners(uc_s.at[j], cells)
-        send_x(fields, UX + j)
-        send_y(uy_s.at[j], uy_r.at[j], UY + j)
-        send_corners(uc_s.at[j], uc_r.at[j], UC + j)
+        send_x(fields, EU + 4 * j)
+        send_y(uy_s.at[j], uy_r.at[j], EU + 4 * j + 2)
+        send_corners(uc_s.at[j], uc_r.at[j], EU + 4 * j + 3)
 
     def take_halo(j):
-        fields = [(u.at[j, 0], 2), (u.at[j, 1], 2)]
-        cells = [(u.at[j, 0], 0, 0), (u.at[j, 1], 0, 0)]
-        take(z.at[4, 0, pl.ds(0, 8 * NYD)], sem_r.at[UX + j])
-        take(uy_r.at[j], sem_r.at[UY + j])
-        take(uc_r.at[j], sem_r.at[UC + j])
-        unpack_y(uy_r.at[j], fields)
+        fields, cells = image_fields(j)
+        take_x(fields, EU + 4 * j)
+        take(uy_r.at[j], sem_r.at[EU + 4 * j + 2])
+        take(uc_r.at[j], sem_r.at[EU + 4 * j + 3])
+        unpack_y(uy_r.at[j], fields, lambda at: True)
         unpack_corners(uc_r.at[j], cells)
 
     def over_own(body):
@@ -551,7 +639,6 @@
 
     columns = []
     lengths = []
-    coarse = []
 
     def finish(j, dots):
         squared = dots[0]
@@ -564,17 +651,18 @@
         lengths.append(jnp.sqrt(squared + epsilon))
 
     for j in range(ITERS):
-        smooth_all(j)
-        start_gather(j, restrict(), products(j))
+        outer(j)
         if j + 1 < ITERS:
             send_halo(j)
         middle_gather(j)
         clear_halo()
+        if j == 0:
+            take_late()
         if j + 1 < ITERS:
             take_halo(j)
-        dots = end_gather(j)
-        coarse.append(coarse_solve(j))
-        finish(j, dots)
+        end_gather(j)
+        coarse_solve(j)
+        finish(j, all_products(j))
         inverse = 1.0 / lengths[j]
         col = columns[j - 1] if j else []
 
@@ -617,6 +705,7 @@
         prolong_own(j)
         over_own(make_image)
         over_own(make_basis)
+        inner(j + 1)
         prolong_halo(j)
         if not last:
             over_halo(2, make_image)
@@ -626,7 +715,7 @@
             if not isinstance(e, int):
                 base = pl.multiple_of(base, 8)
             here = pl.ds(base, 8)
-            parts = [zn[0, here, :], zn[1, here, :]]
+            edge = [zn[0, here, :], zn[1, here, :]]
             for c in range(2):
                 for shift in shifts:
                     beyond = p[c, pl.ds(base + shift, 8), :]
@@ -634,10 +723,10 @@
                         beyond = jnp.where(sub == 7, beyond, 0.0)
                     if shift == -1:
                         beyond = jnp.where(sub == 0, beyond, 0.0)
-                    parts[c] = parts[c] - beyond * inverse
-                zn[c, here, :] = parts[c]
+                    edge[c] = edge[c] - beyond * inverse
+                zn[c, here, :] = edge[c]
             if not last:
-                put_first(here, parts[0], parts[1])
+                put_first(here, edge[0], edge[1])
 
         for e, shift in ((HALO, -PITCH), (HALO + NXD - 1, PITCH)):
             add_edges(e, 0, (shift, -1))
@@ -651,9 +740,8 @@
 
         over_rows(HALO + 1, HALO + NXD - 1, 7, y_edges)
 
-    start_gather(ITERS, None, products(ITERS))
+    outer(ITERS)
     middle_gather(ITERS)
-    finish(ITERS, end_gather(ITERS))
 
     def times(a, b):
         return (a[0] * b[0] - a[1] * b[1], a[0] * b[1] + a[1] * b[0])
@@ -663,7 +751,8 @@
 
     rotations, upper, diagonal = [], [], []
     target = [(lengths[0], zero)]
-    for j in range(ITERS):
+
+    def rotate(j):
         col = list(columns[j])
         for k, (c, s) in enumerate(rotations):
             head, tail = col[k], col[k + 1]
@@ -681,6 +770,11 @@
         last = target[j]
         target[j] = conj_times(c, last)
         target.append((-s * last[0], -s * last[1]))
+    for j in range(ITERS - 1):
+        rotate(j)
+    end_gather(ITERS)
+    finish(ITERS, all_products(ITERS))
+    rotate(ITERS - 1)
     solved = [None] * ITERS
     for j in reversed(range(ITERS)):
         re, im = target[j]
@@ -701,9 +795,11 @@
     c_re, c_im = zero, zero
     for j in range(ITERS):
         wr, wi = weights[j]
-        c_re = c_re + (wr * coarse[j][0] - wi * coarse[j][1])
-        c_im = c_im + (wr * coarse[j][1] + wi * coarse[j][0])
-    table = c_re + pltpu.roll(c_im, 16, axis=1)
+        row = jnp.broadcast_to(cown[j, 0], (8, 128))
+        c_re = c_re + wr * row
+        c_im = c_im + wi * row
+    turned = jnp.where(lane < 16, -pltpu.roll(c_im, 112, axis=1), pltpu.roll(c_im, 16, axis=1))
+    table = jnp.where(lane < 32, c_re + turned, 0.0)
 
     def write(x):
         for t in range(4):
@@ -729,18 +825,20 @@
     hess[0] = h_re[:ITERS, : ITERS + 1]
     hess[1] = h_im[:ITERS, : ITERS + 1]
 
-    take(u.at[0, 0, pl.ds(0, 22 * NYD)], sem_s.at[0])
-    take(iy_s, sem_s.at[1])
-    take(ic_s, sem_s.at[2])
+    for fields, kind, y_out, c_out in ((soon, E0, iy_s, ic_s), (late, E1, ly_s, lc_s)):
+        if kind != E0:
+            take_sent_x(fields, kind)
+        take(y_out, sem_s.at[kind + 2])
+        take(c_out, sem_s.at[kind + 3])
     for j in range(ITERS + 1):
         take(g1.at[j, pl.ds(0, 30)], sem_s.at[S1 + j])
         take(g2.at[j, pl.ds(0, 75)], sem_s.at[S2 + j])
     for j in range(ITERS):
         take(crecv.at[j], sem_s.at[CX + j])
         if j + 1 < ITERS:
-            take(z.at[4, 0, pl.ds(0, 8 * NYD)], sem_s.at[UX + j])
-            take(uy_s.at[j], sem_s.at[UY + j])
-            take(uc_s.at[j], sem_s.at[UC + j])
+            take_sent_x(image_fields(j)[0], EU + 4 * j)
+            take(uy_s.at[j], sem_s.at[EU + 4 * j + 2])
+            take(uc_s.at[j], sem_s.at[EU + 4 * j + 3])
 
 
 def body(*args):
@@ -754,8 +852,8 @@
     solution, hessenberg = pl.pallas_call(
         kernel,
         out_shape=(
-            jax.ShapeDtypeStruct(args[0].shape, F32),
-            jax.ShapeDtypeStruct((2, ITERS, ITERS + 1), F32),
+            pltpu.VMEM(args[0].shape, F32),
+            pltpu.VMEM((2, ITERS, ITERS + 1), F32),
         ),
         in_specs=[pl.BlockSpec(memory_space=pl.ANY)] * 5,
         out_specs=(vmem, vmem),
@@ -765,23 +863,28 @@
             pltpu.VMEM((ROWS, 128), jnp.int32),
             fields(5), fields(4), fields(4), fields(4),
             field, field,
-            pltpu.VMEM((2, NXD, NYD, 128), F32),
+            pltpu.VMEM((2, NXD * NYD, 128), F32),
+            pltpu.VMEM((48, 8, 128), F32),
             pltpu.VMEM((64, 16, 128), F32),
             pltpu.VMEM((64, 16, 128), F32),
             pltpu.VMEM((5, 32, 1, 128), F32),
             pltpu.VMEM((5, 80, 1, 128), F32),
             pltpu.VMEM((4, 1, 1, 128), F32),
             pltpu.VMEM((4, 8, 1, 128), F32),
-            pltpu.VMEM((2, 11, 16, 128), F32),
-            pltpu.VMEM((2, 11, 16, 128), F32),
+            pltpu.VMEM((2, 6, 16, 128), F32),
+            pltpu.VMEM((2, 6, 16, 128), F32),
+            pltpu.VMEM((4, 8, 128), F32),
+            pltpu.VMEM((4, 8, 128), F32),
+            pltpu.VMEM((2, 5, 16, 128), F32),
+            pltpu.VMEM((2, 5, 16, 128), F32),
             pltpu.VMEM((4, 8, 128), F32),
             pltpu.VMEM((4, 8, 128), F32),
             pltpu.VMEM((3, 2, 4, 16, 128), F32),
             pltpu.VMEM((3, 2, 4, 16, 128), F32),
             pltpu.VMEM((3, 4, 8, 128), F32),
             pltpu.VMEM((3, 4, 8, 128), F32),
-            pltpu.SemaphoreType.DMA((28,)),
-            pltpu.SemaphoreType.DMA((28,)),
+            pltpu.SemaphoreType.DMA((34,)),
+            pltpu.SemaphoreType.DMA((34,)),
             pltpu.SemaphoreType.DMA((5,)),
         ],
         compiler_params=pltpu.CompilerParams(

time: 109 us -> 101 us (0.927)
  Pallas kernels: 106 us -> 99.3 us
    pallas_call x1, Pallas kernels: 106 us -> 99.3 us  [body(): pl.pallas_call(kernel, out_shape=(pltpu.VMEM(args[0].shape, F32), pltpu.V...]
    unnamed x4 -> x2, local copies, waits for them, and re-layouts: 2.47 us -> 1.39 us
where the time goes in v3:
time: 101 us
  Pallas kernels  99.3 us (98%)
  local copies, waits for them, and re-layouts  1.39 us (1%)
    pallas_call x1, Pallas kernels, body(): pl.pallas_call(kernel, out_shape=(pltpu.VMEM(args[0].shape, F32), pltpu.V...  99.3 us

profile of v3, /device:TPU:1, one launch (start us, length us, event | category | flops | bytes accessed | tf_op | source)
XLA Modules:
  0.0 101.3 jit_solution(1819033458469876882)
XLA Ops:
  0.6 99.3 %shard_map.68 = (f32[2,16,32,128]{3,2,1,0:T(8,128)S(1)}, f32[2,4,5]{2,1,0:T(4,128)S(1)}) custom-call(f32[2,16,32,128]{3,2,1,0:T(8,128)} %rhs_in.1, f32[16,32,128]{2,1,0:T(8,128)} %wave_in.1, s32[16,32,128]{2,1,0:T(8,128)} %layer_in.1, s32[16,32,128]{2,1,0:T(8,128)} %agg_in.1, f32[2,16,4096]{2,1,0:T(8,128)} %cinv_in.1), custom_call_target="tpu_custom_call" | custom-call | tf_op jit(solution)/shard_map/pallas_call | solution.py:852
  100.0 0.8 copy.9
  100.7 0.6 copy.10

commit v4 on v3

--- a/solution.py
+++ b/solution.py
@@ -320,24 +320,6 @@
         f[0, here, :] = r * a - i * b
         f[1, here, :] = r * b + i * a
 
-    take_x(soon, E0)
-    take(iy_r, sem_r.at[E0 + 2])
-    take(ic_r, sem_r.at[E0 + 3])
-    unpack_y(iy_r, soon, lambda at: at < 4)
-    each_halo(1, lambda e, t: halo_tile(e, t, False, True))
-
-    def halo_first(base):
-        here = pl.ds(base, 8)
-        put_first(here, z[0, 0, here, :], z[0, 1, here, :])
-
-    over_halo(1, halo_first)
-    unpack_y(iy_r, soon, lambda at: at >= 4)
-    for k, (dx, dy) in enumerate(CORNERS):
-        there = x_inside(-1 if dx < 0 else HALO + NXD) * (y_down if dy < 0 else y_up)
-        there = jnp.full((8, 128), there, jnp.int32) > 0
-        ic_r[k] = jnp.where(there, ic_r[k], 0.0)
-    unpack_corners(ic_r, soon_cells)
-
     def take_late():
         take_sent_x(soon, E0)
         take_x(late, E1)
@@ -378,7 +360,6 @@
         over_rows(low, HALO + NXD + width, group, row)
 
     four, five = (0, 1, 2, 3), (0, 1, 2, 3, 4)
-    ALL = [(3, 19, 4, four)]
     INNER_SECOND = [(5, 17, 4, four)]
     OUTER_SECOND = [(2, 5, 3, five), (17, 20, 3, five), (5, 17, 4, (0, 3, 4))]
     INNER_REST = [(6, 16, 5, (1, 2))]
@@ -478,18 +459,12 @@
 
     def outer(j):
         restricted = None
-        if j == 0:
-            over_tiles(1, make_second(0), 3)
-            sweep(ALL, make_rest(0))
-            restricted = sweep_sums(ALL, [zero] * 32, add_restricted)
-            dots = sweep_sums(ALL, [zero], add_products(0))
-        else:
-            if j < ITERS:
-                make_second(j)(row_of(1, 4))
-                sweep(OUTER_SECOND, make_second(j))
-                sweep(OUTER_REST, make_rest(j))
-                restricted = sweep_sums(OUTER_REST, kept(32, 0), add_restricted)
-            dots = sweep_sums(OUTER_DOTS, kept(1 + 2 * j, 32), add_products(j))
+        if j < ITERS:
+            make_second(j)(row_of(1, 4))
+            sweep(OUTER_SECOND, make_second(j))
+            sweep(OUTER_REST, make_rest(j))
+            restricted = sweep_sums(OUTER_REST, kept(32, 0), add_restricted)
+        dots = sweep_sums(OUTER_DOTS, kept(1 + 2 * j, 32), add_products(j))
         if restricted is not None:
             restricted = in_lanes(restricted, lambda k: zl * 16 + (k // 16) * 64 + k % 16)
         start_gather(j, restricted, in_lanes(dots, lambda k: k))
@@ -649,6 +624,25 @@
             squared = jnp.maximum(squared, 0.0)
             columns.append(col)
         lengths.append(jnp.sqrt(squared + epsilon))
+
+    inner(0)
+    take_x(soon, E0)
+    take(iy_r, sem_r.at[E0 + 2])
+    take(ic_r, sem_r.at[E0 + 3])
+    unpack_y(iy_r, soon, lambda at: at < 4)
+    each_halo(1, lambda e, t: halo_tile(e, t, False, True))
+
+    def halo_first(base):
+        here = pl.ds(base, 8)
+        put_first(here, z[0, 0, here, :], z[0, 1, here, :])
+
+    over_halo(1, halo_first)
+    unpack_y(iy_r, soon, lambda at: at >= 4)
+    for k, (dx, dy) in enumerate(CORNERS):
+        known = x_inside(-1 if dx < 0 else HALO + NXD) * (y_down if dy < 0 else y_up)
+        known = jnp.full((8, 128), known, jnp.int32) > 0
+        ic_r[k] = jnp.where(known, ic_r[k], 0.0)
+    unpack_corners(ic_r, soon_cells)
 
     for j in range(ITERS):
         outer(j)

time: 101 us -> 101 us (level)
  no operation moved by 1% of the time
where the time goes in v4:
time: 101 us
  Pallas kernels  98.5 us (98%)
  local copies, waits for them, and re-layouts  1.39 us (1%)
    pallas_call x1, Pallas kernels, body(): pl.pallas_call(kernel, out_shape=(pltpu.VMEM(args[0].shape, F32), pltpu.V...  98.5 us

profile of v4, /device:TPU:1, one launch (start us, length us, event | category | flops | bytes accessed | tf_op | source)
XLA Modules:
  0.0 100.5 jit_solution(13110217057779124621)
XLA Ops:
  0.6 98.5 %shard_map.68 = (f32[2,16,32,128]{3,2,1,0:T(8,128)S(1)}, f32[2,4,5]{2,1,0:T(4,128)S(1)}) custom-call(f32[2,16,32,128]{3,2,1,0:T(8,128)} %rhs_in.1, f32[16,32,128]{2,1,0:T(8,128)} %wave_in.1, s32[16,32,128]{2,1,0:T(8,128)} %layer_in.1, s32[16,32,128]{2,1,0:T(8,128)} %agg_in.1, f32[2,16,4096]{2,1,0:T(8,128)} %cinv_in.1), custom_call_target="tpu_custom_call" | custom-call | tf_op jit(solution)/shard_map/pallas_call | solution.py:846
  99.1 0.8 copy.9
  99.9 0.6 copy.10
